TPU v7x, 32 devices: a whole 2x2x4 slice. The times are simulated.
32 devices in a mesh: view: 4 (over x, core), gz: 8 (over z, y).
Axes of the slice: x: 2, y: 2, z: 4, core: 2. Of those that a mesh axis runs over, the one named last changes fastest.
Arguments:
- views_data: float32 [4, 128, 128, 384], P('view', 'gz'), may hold values from 0.25 to 4
- start: float32 [128, 128, 384], P('gz'), may hold values from 0.5 to 2
- psf_table: float32 [8, 3, 17], replicated, may hold values from 0.05 to 1
- psf_index: int32 [4], P('view'), may hold values from 0 to 7
Outputs:
- estimate: float32 [128, 128, 384], P('gz')
All inputs are finite; a program needn't handle non-finite values.
Results may differ from a plain program's by a relative error of at most 0.0001.
Values sent between devices are 32-bit elements; how exact they have to be, the bound alone decides.
A program may use at most 128 MiB of HBM per device.

v0:
```python
import functools
import jax
import jax.numpy as jnp
from jax import lax
from jax.experimental import pallas as pl
from jax.experimental.pallas import tpu as pltpu
from jax.sharding import PartitionSpec as P

ITERS = 2
AXES = ("view", "gz")
GROUP = 4
VMEM = pl.BlockSpec(memory_space=pltpu.VMEM)
SMEM = pl.BlockSpec(memory_space=pltpu.SMEM)
PARAMS = pltpu.CompilerParams(vmem_limit_bytes=40 * 1024 * 1024)


def split(value):
    high = value.astype(jnp.bfloat16)
    return high, (value - high.astype(jnp.float32)).astype(jnp.bfloat16)


def dot3(lhs, rhs):
    (lh, ll), (rh, rl) = lhs, rhs
    dot = functools.partial(jnp.dot, preferred_element_type=jnp.float32)
    return dot(lh, rh) + (dot(ll, rh) + dot(lh, rl))


def taps_sum(kz_ref, source, flip):
    taps = kz_ref.shape[0]
    total = kz_ref[taps - 1 if flip else 0] * source(0)
    for tap in range(1, taps):
        total = total + kz_ref[taps - 1 - tap if flip else tap] * source(tap)
    return total


def forward_kernel(kz_ref, e_ref, d_ref, ax_ref, my_ref, r_ref, zc_ref):
    rows_in, width = e_ref.shape[1], e_ref.shape[2]
    rows = d_ref.shape[1]
    ax = split(ax_ref[...])
    my = split(my_ref[...])

    @pl.loop(0, d_ref.shape[0] // GROUP)
    def _(step):
        base = step * GROUP
        for plane in range(GROUP):
            for tile in range(rows_in // 8):
                at = pl.ds(tile * 8, 8)
                zc_ref[pl.ds(plane * rows_in + tile * 8, 8), :] = taps_sum(
                    kz_ref, lambda tap: e_ref[base + plane + tap, at, :], False
                )
        along_x = dot3(ax, split(zc_ref[...]))
        blurred = dot3(split(along_x), my)
        r_ref[pl.ds(base, GROUP)] = d_ref[pl.ds(base, GROUP)] / blurred.reshape(GROUP, rows, width)


def smear_kernel(kz_ref, low_ref, r_ref, high_ref, u_ref):
    planes, pad = r_ref.shape[0], low_ref.shape[0]

    def source(place):
        if place < pad:
            return low_ref[place]
        if place < pad + planes:
            return r_ref[place - pad]
        return high_ref[place - pad - planes]

    for plane in range(planes):
        u_ref[plane] = taps_sum(kz_ref, lambda tap: source(plane + tap), True)


def back_kernel(low_ref, u_ref, high_ref, ax_ref, my_ref, *rest):
    out_ref, wide_ref = rest[-2:]
    rows, width = u_ref.shape[1], u_ref.shape[2]
    pad = low_ref.shape[1]
    wide = rows + 2 * pad
    ax = split(ax_ref[...])
    my = split(my_ref[...])

    @pl.loop(0, u_ref.shape[0] // GROUP)
    def _(step):
        base = step * GROUP
        for plane in range(GROUP):
            wide_ref[pl.ds(plane * wide, pad), :] = low_ref[base + plane]
            wide_ref[pl.ds(plane * wide + pad, rows), :] = u_ref[base + plane]
            wide_ref[pl.ds(plane * wide + pad + rows, pad), :] = high_ref[base + plane]
        along_x = dot3(ax, split(wide_ref[...]))
        result = dot3(split(along_x), my).reshape(GROUP, rows, width)
        if len(rest) == 3:
            result = result * rest[0][pl.ds(base, GROUP)]
        out_ref[pl.ds(base, GROUP)] = result


def blur_forward(kz, wide, data, ax, my):
    planes, rows, width = data.shape
    return pl.pallas_call(
        forward_kernel,
        out_shape=jax.ShapeDtypeStruct(data.shape, jnp.float32),
        in_specs=[SMEM, VMEM, VMEM, VMEM, VMEM],
        out_specs=VMEM,
        scratch_shapes=[pltpu.VMEM((GROUP * wide.shape[1], width), jnp.float32)],
        compiler_params=PARAMS,
        cost_estimate=pl.CostEstimate(
            flops=data.size * 2 * width * 12, bytes_accessed=16 * data.size, transcendentals=0
        ),
    )(kz, wide, data, ax, my)


def smear(kz, low, ratio, high):
    planes, rows, width = ratio.shape
    pad = low.shape[0]
    block = lambda depth: pl.BlockSpec((depth, 8, width), lambda i: (0, i, 0))
    return pl.pallas_call(
        smear_kernel,
        grid=(rows // 8,),
        out_shape=jax.ShapeDtypeStruct(ratio.shape, jnp.float32),
        in_specs=[SMEM, block(pad), block(planes), block(pad)],
        out_specs=block(planes),
        compiler_params=PARAMS,
        cost_estimate=pl.CostEstimate(
            flops=ratio.size * 2 * width * 6, bytes_accessed=12 * ratio.size, transcendentals=0
        ),
    )(kz, low, ratio, high)


def blur_back(low, u, high, ax, my, other):
    planes, rows, width = u.shape
    extra = [] if other is None else [other]
    return pl.pallas_call(
        back_kernel,
        out_shape=jax.ShapeDtypeStruct(u.shape, jnp.float32),
        in_specs=[VMEM] * (5 + len(extra)),
        out_specs=VMEM,
        scratch_shapes=[pltpu.VMEM((GROUP * (rows + 2 * low.shape[1]), width), jnp.float32)],
        compiler_params=PARAMS,
        cost_estimate=pl.CostEstimate(
            flops=u.size * 2 * width * 6, bytes_accessed=12 * u.size, transcendentals=0
        ),
    )(low, u, high, ax, my, *extra)


def banded(kern_row, outputs, inputs, shift):
    tap = jnp.arange(inputs)[None, :] - jnp.arange(outputs)[:, None] + shift
    taps = jnp.arange(kern_row.shape[0])
    return jnp.sum(jnp.where(tap[None] == taps[:, None, None], kern_row[:, None, None], 0.0), axis=0)


def x_matrix(kern_row, rows, pad):
    one = banded(kern_row, rows, rows + 2 * pad, 0)
    eye = jnp.eye(GROUP, dtype=jnp.float32)
    return (eye[:, None, :, None] * one[None, :, None, :]).reshape(
        GROUP * rows, GROUP * (rows + 2 * pad)
    )


def on_device(sections, count, views_data, start, psf_table, psf_index):
    slab = views_data[0]
    planes, width_x, width_y = start.shape
    pad = (psf_table.shape[2] - 1) // 2
    share = width_x // 4
    half = planes // 2
    view, gz = lax.axis_index("view"), lax.axis_index("gz")
    a, c, b = view // 2, view % 2, gz % 2

    def strip_of(a, b):
        return 2 * a + (a + b) % 2

    def move(value, target):
        pairs = []
        for v in range(sections):
            for g in range(count):
                to = target(v // 2, v % 2, g // 2, g % 2)
                if to is not None:
                    pairs.append((v * count + g, (2 * to[0] + to[1]) * count + 2 * to[2] + to[3]))
        return lax.ppermute(value, AXES, pairs)

    def along_z(step):
        def target(a, c, k, b):
            return (a, c, k + step, b) if 0 <= k + step < count // 2 else None

        return target

    def along_x(step):
        def target(a, c, k, b):
            strip = strip_of(a, b) + step
            if not 0 <= strip < 4:
                return None
            return (strip // 2, c, k, (strip % 2 + strip // 2) % 2)

        return target

    partners = (
        lambda a, c, k, b: (a, c, k, 1 - b),
        lambda a, c, k, b: (1 - a, c, k, b),
        lambda a, c, k, b: (1 - a, c, k, 1 - b),
    )
    core_swap = lambda a, c, k, b: (a, 1 - c, k, b)

    def rows_for(block, a, b):
        return lax.dynamic_slice_in_dim(block, strip_of(a, b) * share, share, 1)

    def in_order(first_is_mine, mine, theirs):
        return jnp.concatenate(
            [jnp.where(first_is_mine, mine, theirs), jnp.where(first_is_mine, theirs, mine)], axis=0
        )

    kern = jnp.sum(jnp.where(jnp.arange(psf_table.shape[0])[:, None, None] == psf_index[0], psf_table, 0.0), axis=0)
    kern = kern / jnp.sum(kern, axis=-1, keepdims=True)
    other = move(kern, partners[1])
    kerns = (jnp.where(a == 0, kern, other), jnp.where(a == 0, other, kern))
    setups = []
    for kern in kerns:
        flipped = kern[:, ::-1]
        mat_y = banded(kern[2], width_y, width_y, pad)
        setups.append((
            kern[0], x_matrix(kern[1], share, pad), mat_y.T, x_matrix(flipped[1], share, pad), mat_y
        ))

    theirs = rows_for(start, a, 1 - b)
    part = move(lax.dynamic_slice_in_dim(theirs, c * half, half, 0), partners[0])
    theirs = in_order(c == 0, part, move(part, core_swap))
    estimate = in_order(b == 0, rows_for(start, a, b), theirs)

    mine = rows_for(slab, a, b)
    from_y = move(rows_for(slab, a, 1 - b), partners[0])
    from_x = move(rows_for(slab, 1 - a, b), partners[1])
    from_xy = move(rows_for(slab, 1 - a, 1 - b), partners[2])
    data = tuple(
        in_order(b == 0, jnp.where(a == high, mine, from_x), jnp.where(a == high, from_y, from_xy))
        for high in range(2)
    )

    for step in range(ITERS):
        low = move(estimate[:, share - pad:], along_x(1))
        high = move(estimate[:, :pad], along_x(-1))
        wide = jnp.concatenate([low, estimate, high], axis=1)
        low = move(wide[2 * planes - pad:], along_z(1))
        high = move(wide[:pad], along_z(-1))
        wide = jnp.concatenate([low, wide, high], axis=0)
        smeared = []
        for which in range(2):
            kz, ax, my = setups[which][:3]
            ratio = blur_forward(kz, wide, data[which], ax, my)
            low = move(ratio[2 * planes - pad:], along_z(1))
            high = move(ratio[:pad], along_z(-1))
            smeared.append((low, ratio, high))
        edges = []
        for which in range(2):
            u = smear(setups[which][0], *smeared[which])
            low = move(u[:, share - pad:], along_x(1))
            high = move(u[:, :pad], along_x(-1))
            edges.append((low, u, high))
        product = None
        for which in range(2):
            ax, my = setups[which][3:]
            product = blur_back(*edges[which], ax, my, product)
        total = product * move(product, core_swap)
        estimate = estimate * jnp.sqrt(jnp.sqrt(total))

    def piece(b):
        return lax.dynamic_slice_in_dim(estimate, planes * b + half * c, half, 0)

    got = (
        piece(b),
        move(piece(1 - b), partners[0]),
        move(piece(b), partners[1]),
        move(piece(1 - b), partners[2]),
    )
    strips = []
    for strip in range(4):
        at_a = strip // 2
        at_b = (strip % 2 + at_a) % 2
        same_a, same_b = a == at_a, b == at_b
        strips.append(jnp.where(
            same_a, jnp.where(same_b, got[0], got[1]), jnp.where(same_b, got[2], got[3])
        ))
    whole = jnp.concatenate(strips, axis=1)
    return in_order(c == 0, whole, move(whole, core_swap))


def solution(mesh):
    return jax.shard_map(
        functools.partial(on_device, mesh.shape["view"], mesh.shape["gz"]),
        mesh=mesh,
        in_specs=(P("view", "gz", None, None), P("gz", None, None), P(), P("view")),
        out_specs=P("gz", None, None),
        check_vma=False,
    )
```

profile of v0, /device:TPU:17, one launch (start us, length us, event | category | flops | bytes accessed | tf_op | source)
XLA Modules:
  0.0 274.4 jit_solution(1236903080191966282)
XLA Ops:
  3.9 1.3 collective-permute-start
  5.2 3.1 %dynamic-slice_bitcast_fusion.2 = (f32[16,32,384]{2,1,0:T(8,128)}, f32[16,32,384]{2,1,0:T(8,128)}, f32[16,32,384]{2,1,0:T(8,128)}) fusion(f32[1,16,128,384]{3,2,1,0:T(8,128)} %param.4, s32[]{:T(128)S(6)} %select_n.244, s32[]{:T(128)S(6)} %select_n.247, s32[]{:T(128)S(6)} %select_n.233), kind=kLoop, calls=%fused_computation.21 | loop fusion | bytes 4718604 | tf_op jit(solution)/shard_map/dynamic_slice | solution.py:198
  11.0 2.7 collective-permute-done
  13.7 3.2 %collective-permute-start.1 = (f32[8,32,384]{2,1,0:T(8,128)S(1)}, f32[8,32,384]{2,1,0:T(8,128)S(1)}, u32[]{:S(2)}, u32[]{:S(2)}) collective-permute-start(f32[8,32,384]{2,1,0:T(8,128)S(1)} %collective-permute-done), channel_id=1, source_target_pairs={{0,8},{1,9},{2,10},{3,11},{4,12},{5,13},{6,14},{7,15},{8,0},{9,1},... | collective-permute-start | bytes 1179656 | tf_op jit(solution)/shard_map/ppermute | solution.py:173
  18.3 1.3 dynamic-slice_select_fusion.1
  19.7 3.2 %collective-permute-start.3 = (f32[32,8,384]{2,1,0:T(8,128)S(1)}, f32[32,8,384]{2,1,0:T(8,128)S(1)}, u32[]{:S(2)}, u32[]{:S(2)}) collective-permute-start(f32[32,8,384]{2,1,0:T(8,128)S(1)} %get-tuple-element.52), channel_id=1, source_target_pairs={{0,1},{1,17},{2,3},{3,19},{4,5},{5,21},{6,7},{7,23},{8,9},{9,25},{... | collective-permute-start | bytes 1179656 | tf_op jit(solution)/shard_map/ppermute | solution.py:173
  22.9 1.3 collective-permute-start.4
  24.2 1.7 select_reduce_fusion
  25.9 29.0 %collective-permute-done.3 = f32[32,8,384]{2,1,0:T(8,128)S(1)} collective-permute-done((f32[32,8,384]{2,1,0:T(8,128)S(1)}, f32[32,8,384]{2,1,0:T(8,128)S(1)}, u32[]{:S(2)}, u32[]{:S(2)}) %collective-permute-start.3) | collective-permute-done | bytes 393248 | tf_op jit(solution)/shard_map/ppermute | solution.py:173
  57.1 3.2 %collective-permute-start.5 = (f32[8,48,384]{2,1,0:T(8,128)}, f32[8,48,384]{2,1,0:T(8,128)}, u32[]{:S(2)}, u32[]{:S(2)}) collective-permute-start(f32[8,48,384]{2,1,0:T(8,128)} %get-tuple-element.26), channel_id=1, source_target_pairs={{0,2},{1,3},{2,4},{3,5},{4,6},{5,7},{8,10},{9,11},{10,12},{11,13},... | collective-permute-start | bytes 1769480 | tf_op jit(solution)/shard_map/ppermute | solution.py:173
  60.3 2.1 collective-permute-start.6
  65.7 2.0 broadcast_select_fusion.5
  68.0 4.4 %collective-permute-done.5 = f32[8,48,384]{2,1,0:T(8,128)} collective-permute-done((f32[8,48,384]{2,1,0:T(8,128)}, f32[8,48,384]{2,1,0:T(8,128)}, u32[]{:S(2)}, u32[]{:S(2)}) %collective-permute-start.5) | collective-permute-done | bytes 589856 | tf_op jit(solution)/shard_map/ppermute | solution.py:173
  72.3 2.9 %collective-permute-done.6 = f32[8,48,384]{2,1,0:T(8,128)} collective-permute-done((f32[8,48,384]{2,1,0:T(8,128)}, f32[8,48,384]{2,1,0:T(8,128)}, u32[]{:S(2)}, u32[]{:S(2)}) %collective-permute-start.6) | collective-permute-done | bytes 589856 | tf_op jit(solution)/shard_map/ppermute | solution.py:173
  75.3 1.5 pad_maximum_fusion.e_ref
  76.8 7.8 %shard_map.48.r_ref = f32[32,32,384]{2,1,0:T(8,128)S(1)} custom-call(f32[17]{0:T(128)S(1)} %get-tuple-element.62.kz_ref, f32[48,48,384]{2,1,0:T(8,128)S(1)} %pad_maximum_fusion.e_ref, f32[32,32,384]{2,1,0:T(8,128)S(1)} %get-tuple-element.75.d_ref, f32[128,192]{1,0:T(8,128)S(1)} %copy-done.8, f32[384,384]{1,0:T(8,128)S(1)} %bitcast.37), custom_call_target="tpu_custom_call" | custom-call | flops 3623878656 | bytes 6291456 | tf_op jit(solution)/shard_map/pallas_call | solution.py:94
  84.7 2.1 collective-permute-start.15
  86.8 3.2 %collective-permute-start.14 = (f32[8,32,384]{2,1,0:T(8,128)S(1)}, f32[8,32,384]{2,1,0:T(8,128)S(1)}, u32[]{:S(2)}, u32[]{:S(2)}) collective-permute-start(f32[8,32,384]{2,1,0:T(8,128)S(1)} %get-tuple-element.47), channel_id=1, source_target_pairs={{0,2},{1,3},{2,4},{3,5},{4,6},{5,7},{8,10},{9,11},{10,12},{11,13},... | collective-permute-start | bytes 1179656 | tf_op jit(solution)/shard_map/ppermute | solution.py:173
  90.0 7.8 %shard_map.46.r_ref = f32[32,32,384]{2,1,0:T(8,128)S(1)} custom-call(f32[17]{0:T(128)S(1)} %get-tuple-element.70.kz_ref, f32[48,48,384]{2,1,0:T(8,128)S(1)} %pad_maximum_fusion.e_ref, f32[32,32,384]{2,1,0:T(8,128)S(1)} %get-tuple-element.74.d_ref, f32[128,192]{1,0:T(8,128)S(1)} %mul.129.ax_ref, f32[384,384]{1,0:T(8,128)S(1)} %bitcast.35), custom_call_target="tpu_custom_call" | custom-call | flops 3623878656 | bytes 6291456 | tf_op jit(solution)/shard_map/pallas_call | solution.py:94
  98.0 2.1 collective-permute-start.11
  100.0 3.2 %collective-permute-start.10 = (f32[8,32,384]{2,1,0:T(8,128)S(1)}, f32[8,32,384]{2,1,0:T(8,128)S(1)}, u32[]{:S(2)}, u32[]{:S(2)}) collective-permute-start(f32[8,32,384]{2,1,0:T(8,128)S(1)} %get-tuple-element.51), channel_id=1, source_target_pairs={{0,2},{1,3},{2,4},{3,5},{4,6},{5,7},{8,10},{9,11},{10,12},{11,13},... | collective-permute-start | bytes 1179656 | tf_op jit(solution)/shard_map/ppermute | solution.py:173
  103.3 2.7 shard_map.49.u_ref
  108.1 1.3 collective-permute-start.17
  109.4 4.8 %collective-permute-start.16 = (f32[32,8,384]{2,1,0:T(8,128)}, f32[32,8,384]{2,1,0:T(8,128)}, u32[]{:S(2)}, u32[]{:S(2)}) collective-permute-start(f32[32,8,384]{2,1,0:T(8,128)} %get-tuple-element.45), channel_id=1, source_target_pairs={{0,1},{1,17},{2,3},{3,19},{4,5},{5,21},{6,7},{7,23},{8,9},{9,25},{... | collective-permute-start | bytes 1179656 | tf_op jit(solution)/shard_map/ppermute | solution.py:173
  114.2 2.7 shard_map.47.u_ref
  118.9 1.3 collective-permute-start.13
  120.2 4.7 %collective-permute-start.12 = (f32[32,8,384]{2,1,0:T(8,128)}, f32[32,8,384]{2,1,0:T(8,128)}, u32[]{:S(2)}, u32[]{:S(2)}) collective-permute-start(f32[32,8,384]{2,1,0:T(8,128)} %get-tuple-element.49), channel_id=1, source_target_pairs={{0,1},{1,17},{2,3},{3,19},{4,5},{5,21},{6,7},{7,23},{8,9},{9,25},{... | collective-permute-start | bytes 1179656 | tf_op jit(solution)/shard_map/ppermute | solution.py:173
  125.0 1.8 mul.138.ax_ref
  126.7 1.8 mul.132.ax_ref
  128.5 1.4 copy-done.5
  130.8 5.8 %shard_map.50.rest_0_ = f32[32,32,384]{2,1,0:T(8,128)S(1)} custom-call(f32[32,8,384]{2,1,0:T(8,128)} %collective-permute-done.16.low_ref, f32[32,32,384]{2,1,0:T(8,128)S(1)} %copy-done.5, f32[32,8,384]{2,1,0:T(8,128)} %collective-permute-done.17.high_ref, f32[128,192]{1,0:T(8,128)S(1)} %copy-done.11, f32[384,384]{1,0:T(8,128)S(1)} %get-tuple-element.5.my_ref), custom_call_target="tpu_custom_call" | custom-call | flops 1811939328 | bytes 4718592 | tf_op jit(solution)/shard_map/pallas_call | solution.py:127
  136.7 5.8 %shard_map.51 = f32[32,32,384]{2,1,0:T(8,128)S(1)} custom-call(f32[32,8,384]{2,1,0:T(8,128)} %collective-permute-done.12.low_ref, f32[32,32,384]{2,1,0:T(8,128)S(1)} %copy-done.7, f32[32,8,384]{2,1,0:T(8,128)} %collective-permute-done.13.high_ref, f32[128,192]{1,0:T(8,128)S(1)} %copy-done.10, f32[384,384]{1,0:T(8,128)S(1)} %get-tuple-element.6.my_ref, ...), custom_call_target="tpu_custom_call" | custom-call | flops 1811939328 | bytes 4718592 | tf_op jit(solution)/shard_map/pallas_call | solution.py:127
  142.6 5.3 %collective-permute-start.18 = (f32[32,32,384]{2,1,0:T(8,128)S(1)}, f32[32,32,384]{2,1,0:T(8,128)S(1)}, u32[]{:S(2)}, u32[]{:S(2)}) collective-permute-start(f32[32,32,384]{2,1,0:T(8,128)S(1)} %shard_map.51), channel_id=1, source_target_pairs={{0,8},{1,9},{2,10},{3,11},{4,12},{5,13},{6,14},{7,15},{8,0},{9,1},... | collective-permute-start | bytes 4718600 | tf_op jit(solution)/shard_map/ppermute | solution.py:173
  147.8 3.0 %collective-permute-done.18 = f32[32,32,384]{2,1,0:T(8,128)S(1)} collective-permute-done((f32[32,32,384]{2,1,0:T(8,128)S(1)}, f32[32,32,384]{2,1,0:T(8,128)S(1)}, u32[]{:S(2)}, u32[]{:S(2)}) %collective-permute-start.18) | collective-permute-done | bytes 1572896 | tf_op jit(solution)/shard_map/ppermute | solution.py:173
  151.8 2.0 collective-permute-start.19
  153.8 1.3 collective-permute-start.20
  155.1 6.8 %collective-permute-done.19 = f32[32,8,384]{2,1,0:T(8,128)S(1)} collective-permute-done((f32[32,8,384]{2,1,0:T(8,128)S(1)}, f32[32,8,384]{2,1,0:T(8,128)S(1)}, u32[]{:S(2)}, u32[]{:S(2)}) %collective-permute-start.19) | collective-permute-done | bytes 393248 | tf_op jit(solution)/shard_map/ppermute | solution.py:173
  161.8 4.2 %collective-permute-done.20 = f32[32,8,384]{2,1,0:T(8,128)S(1)} collective-permute-done((f32[32,8,384]{2,1,0:T(8,128)S(1)}, f32[32,8,384]{2,1,0:T(8,128)S(1)}, u32[]{:S(2)}, u32[]{:S(2)}) %collective-permute-start.20) | collective-permute-done | bytes 393248 | tf_op jit(solution)/shard_map/ppermute | solution.py:173
  166.1 1.9 collective-permute-start.21
  168.0 3.5 %collective-permute-start.22 = (f32[8,48,384]{2,1,0:T(8,128)S(1)}, f32[8,48,384]{2,1,0:T(8,128)S(1)}, u32[]{:S(2)}, u32[]{:S(2)}) collective-permute-start(f32[8,48,384]{2,1,0:T(8,128)S(1)} %get-tuple-element.25), channel_id=1, source_target_pairs={{2,0},{3,1},{4,2},{5,3},{6,4},{7,5},{10,8},{11,9},{12,10},{13,11},... | collective-permute-start | bytes 1769480 | tf_op jit(solution)/shard_map/ppermute | solution.py:173
  171.5 10.0 %collective-permute-done.21 = f32[8,48,384]{2,1,0:T(8,128)S(1)} collective-permute-done((f32[8,48,384]{2,1,0:T(8,128)S(1)}, f32[8,48,384]{2,1,0:T(8,128)S(1)}, u32[]{:S(2)}, u32[]{:S(2)}) %collective-permute-start.21) | collective-permute-done | bytes 589856 | tf_op jit(solution)/shard_map/ppermute | solution.py:173
  181.5 2.1 collective-permute-done.22
  183.9 7.8 %shard_map.54.r_ref = f32[32,32,384]{2,1,0:T(8,128)S(1)} custom-call(f32[17]{0:T(128)S(1)} %get-tuple-element.62.kz_ref, f32[48,48,384]{2,1,0:T(8,128)S(1)} %pad_maximum_fusion.1.e_ref, f32[32,32,384]{2,1,0:T(8,128)S(1)} %copy-done.1, f32[128,192]{1,0:T(8,128)S(1)} %copy-done.9, f32[384,384]{1,0:T(8,128)S(1)} %bitcast.38), custom_call_target="tpu_custom_call" | custom-call | flops 3623878656 | bytes 6291456 | tf_op jit(solution)/shard_map/pallas_call | solution.py:94
  191.8 3.1 %collective-permute-start.28 = (f32[8,32,384]{2,1,0:T(8,128)S(1)}, f32[8,32,384]{2,1,0:T(8,128)S(1)}, u32[]{:S(2)}, u32[]{:S(2)}) collective-permute-start(f32[8,32,384]{2,1,0:T(8,128)S(1)} %get-tuple-element.36), channel_id=1, source_target_pairs={{2,0},{3,1},{4,2},{5,3},{6,4},{7,5},{10,8},{11,9},{12,10},{13,11},... | collective-permute-start | bytes 1179656 | tf_op jit(solution)/shard_map/ppermute | solution.py:173
  194.9 2.2 collective-permute-start.27
  197.1 7.8 %shard_map.52.r_ref = f32[32,32,384]{2,1,0:T(8,128)S(1)} custom-call(f32[17]{0:T(128)S(1)} %get-tuple-element.70.kz_ref, f32[48,48,384]{2,1,0:T(8,128)S(1)} %pad_maximum_fusion.1.e_ref, f32[32,32,384]{2,1,0:T(8,128)S(1)} %get-tuple-element.74.d_ref, f32[128,192]{1,0:T(8,128)S(1)} %mul.129.ax_ref, f32[384,384]{1,0:T(8,128)S(1)} %bitcast.36), custom_call_target="tpu_custom_call" | custom-call | flops 3623878656 | bytes 6291456 | tf_op jit(solution)/shard_map/pallas_call | solution.py:94
  205.0 3.1 %collective-permute-start.24 = (f32[8,32,384]{2,1,0:T(8,128)S(1)}, f32[8,32,384]{2,1,0:T(8,128)S(1)}, u32[]{:S(2)}, u32[]{:S(2)}) collective-permute-start(f32[8,32,384]{2,1,0:T(8,128)S(1)} %get-tuple-element.40), channel_id=1, source_target_pairs={{2,0},{3,1},{4,2},{5,3},{6,4},{7,5},{10,8},{11,9},{12,10},{13,11},... | collective-permute-start | bytes 1179656 | tf_op jit(solution)/shard_map/ppermute | solution.py:173
  208.1 2.2 collective-permute-start.23
  210.3 2.7 shard_map.55.u_ref
  213.1 1.3 collective-permute-start.30
  214.4 4.0 %collective-permute-start.29 = (f32[32,8,384]{2,1,0:T(8,128)S(1)}, f32[32,8,384]{2,1,0:T(8,128)S(1)}, u32[]{:S(2)}, u32[]{:S(2)}) collective-permute-start(f32[32,8,384]{2,1,0:T(8,128)S(1)} %get-tuple-element.35), channel_id=1, source_target_pairs={{0,1},{1,17},{2,3},{3,19},{4,5},{5,21},{6,7},{7,23},{8,9},{9,25},{... | collective-permute-start | bytes 1179656 | tf_op jit(solution)/shard_map/ppermute | solution.py:173
  218.4 2.7 shard_map.53.u_ref
  221.2 1.3 collective-permute-start.26
  222.5 4.0 %collective-permute-start.25 = (f32[32,8,384]{2,1,0:T(8,128)S(1)}, f32[32,8,384]{2,1,0:T(8,128)S(1)}, u32[]{:S(2)}, u32[]{:S(2)}) collective-permute-start(f32[32,8,384]{2,1,0:T(8,128)S(1)} %get-tuple-element.39), channel_id=1, source_target_pairs={{0,1},{1,17},{2,3},{3,19},{4,5},{5,21},{6,7},{7,23},{8,9},{9,25},{... | collective-permute-start | bytes 1179656 | tf_op jit(solution)/shard_map/ppermute | solution.py:173
  226.5 4.6 %shard_map.56.rest_0_ = f32[32,32,384]{2,1,0:T(8,128)S(1)} custom-call(f32[32,8,384]{2,1,0:T(8,128)S(1)} %collective-permute-done.29.low_ref, f32[32,32,384]{2,1,0:T(8,128)S(1)} %shard_map.55.u_ref, f32[32,8,384]{2,1,0:T(8,128)S(1)} %collective-permute-done.30.high_ref, f32[128,192]{1,0:T(8,128)S(1)} %copy-done.12, f32[384,384]{1,0:T(8,128)S(1)} %get-tuple-element.5.my_ref), custom_call_target="tpu_custom_call" | custom-call | flops 1811939328 | bytes 4718592 | tf_op jit(solution)/shard_map/pallas_call | solution.py:127
  231.5 4.6 %shard_map.57 = f32[32,32,384]{2,1,0:T(8,128)S(1)} custom-call(f32[32,8,384]{2,1,0:T(8,128)S(1)} %collective-permute-done.25.low_ref, f32[32,32,384]{2,1,0:T(8,128)S(1)} %shard_map.53.u_ref, f32[32,8,384]{2,1,0:T(8,128)S(1)} %collective-permute-done.26.high_ref, f32[128,192]{1,0:T(8,128)S(1)} %copy-done.10, f32[384,384]{1,0:T(8,128)S(1)} %get-tuple-element.6.my_ref, ...), custom_call_target="tpu_custom_call" | custom-call | flops 1811939328 | bytes 4718592 | tf_op jit(solution)/shard_map/pallas_call | solution.py:127
  236.1 4.8 %collective-permute-start.31 = (f32[32,32,384]{2,1,0:T(8,128)S(1)}, f32[32,32,384]{2,1,0:T(8,128)}, u32[]{:S(2)}, u32[]{:S(2)}) collective-permute-start(f32[32,32,384]{2,1,0:T(8,128)S(1)} %shard_map.57), channel_id=1, source_target_pairs={{0,8},{1,9},{2,10},{3,11},{4,12},{5,13},{6,14},{7,15},{8,0},{9,1},... | collective-permute-start | bytes 4718600 | tf_op jit(solution)/shard_map/ppermute | solution.py:173
  240.9 3.2 %collective-permute-done.31 = f32[32,32,384]{2,1,0:T(8,128)} collective-permute-done((f32[32,32,384]{2,1,0:T(8,128)S(1)}, f32[32,32,384]{2,1,0:T(8,128)}, u32[]{:S(2)}, u32[]{:S(2)}) %collective-permute-start.31) | collective-permute-done | bytes 1572896 | tf_op jit(solution)/shard_map/ppermute | solution.py:173
  244.1 2.7 sqrt_multiply_fusion
  246.8 3.3 %collective-permute-start.34 = (f32[8,32,384]{2,1,0:T(8,128)S(1)}, f32[8,32,384]{2,1,0:T(8,128)S(1)}, u32[]{:S(2)}, u32[]{:S(2)}) collective-permute-start(f32[8,32,384]{2,1,0:T(8,128)S(1)} %get-tuple-element.32), channel_id=1, source_target_pairs={{0,17},{1,16},{2,19},{3,18},{4,21},{5,20},{6,23},{7,22},{8,25},{9,... | collective-permute-start | bytes 1179656 | tf_op jit(solution)/shard_map/ppermute | solution.py:173
  250.5 8.8 %collective-permute-done.34 = f32[8,32,384]{2,1,0:T(8,128)S(1)} collective-permute-done((f32[8,32,384]{2,1,0:T(8,128)S(1)}, f32[8,32,384]{2,1,0:T(8,128)S(1)}, u32[]{:S(2)}, u32[]{:S(2)}) %collective-permute-start.34) | collective-permute-done | bytes 393248 | tf_op jit(solution)/shard_map/ppermute | solution.py:173
  259.2 8.8 %collective-permute-done.32 = f32[8,32,384]{2,1,0:T(8,128)S(1)} collective-permute-done((f32[8,32,384]{2,1,0:T(8,128)S(1)}, f32[8,32,384]{2,1,0:T(8,128)S(1)}, u32[]{:S(2)}, u32[]{:S(2)}) %collective-permute-start.32) | collective-permute-done | bytes 393248 | tf_op jit(solution)/shard_map/ppermute | solution.py:173
  269.2 3.0 %collective-permute-done.35 = f32[8,128,384]{2,1,0:T(8,128)S(1)} collective-permute-done((f32[8,128,384]{2,1,0:T(8,128)S(1)}, f32[8,128,384]{2,1,0:T(8,128)S(1)}, u32[]{:S(2)}, u32[]{:S(2)}) %collective-permute-start.35) | collective-permute-done | bytes 1572896 | tf_op jit(solution)/shard_map/ppermute | solution.py:173
  272.5 1.9 pad_maximum_fusion.2
  (114 shorter events, 22.1 us)
Async XLA Ops:
  1.6 15.3 %collective-permute-start.2 = (f32[3,17]{1,0:T(4,128)S(1)}, f32[3,17]{1,0:T(4,128)S(1)}, u32[]{:S(2)}, u32[]{:S(2)}) collective-permute-start(f32[3,17]{1,0:T(4,128)S(1)} %broadcast_divide_fusion), channel_id=1, source_target_pairs={{0,16},{1,17},{2,18},{3,19},{4,20},{5,21},{6,22},{7,23},{8,24},{9,... | collective-permute-start | bytes 620 | tf_op jit(solution)/shard_map/ppermute | solution.py:173
  3.9 9.8 %collective-permute-start = (f32[8,32,384]{2,1,0:T(8,128)S(1)}, f32[8,32,384]{2,1,0:T(8,128)S(1)}, u32[]{:S(2)}, u32[]{:S(2)}) collective-permute-start(f32[8,32,384]{2,1,0:T(8,128)S(1)} %constant_dynamic-slice_fusion.2), channel_id=1, source_target_pairs={{0,1},{1,0},{2,3},{3,2},{4,5},{5,4},{6,7},{7,6},{8,9},{9,8},{10,11... | collective-permute-start | bytes 1179656 | tf_op jit(solution)/shard_map/ppermute | solution.py:173
  8.3 57.3 %collective-permute-start.7 = (f32[16,32,384]{2,1,0:T(8,128)}, f32[16,32,384]{2,1,0:T(8,128)S(1)}, u32[]{:S(2)}, u32[]{:S(2)}) collective-permute-start(f32[16,32,384]{2,1,0:T(8,128)} %get-tuple-element.21), channel_id=1, source_target_pairs={{0,16},{1,17},{2,18},{3,19},{4,20},{5,21},{6,22},{7,23},{8,24},{9,... | collective-permute-start | bytes 2359304 | tf_op jit(solution)/shard_map/ppermute | solution.py:173
  8.5 57.1 %collective-permute-start.9 = (f32[16,32,384]{2,1,0:T(8,128)}, f32[16,32,384]{2,1,0:T(8,128)}, u32[]{:S(2)}, u32[]{:S(2)}) collective-permute-start(f32[16,32,384]{2,1,0:T(8,128)} %get-tuple-element.22), channel_id=1, source_target_pairs={{0,17},{1,16},{2,19},{3,18},{4,21},{5,20},{6,23},{7,22},{8,25},{9,... | collective-permute-start | bytes 2359304 | tf_op jit(solution)/shard_map/ppermute | solution.py:173
  9.7 56.0 %collective-permute-start.8 = (f32[16,32,384]{2,1,0:T(8,128)}, f32[16,32,384]{2,1,0:T(8,128)}, u32[]{:S(2)}, u32[]{:S(2)}) collective-permute-start(f32[16,32,384]{2,1,0:T(8,128)} %get-tuple-element.23), channel_id=1, source_target_pairs={{0,1},{1,0},{2,3},{3,2},{4,5},{5,4},{6,7},{7,6},{8,9},{9,8},{10,11... | collective-permute-start | bytes 2359304 | tf_op jit(solution)/shard_map/ppermute | solution.py:173
  13.7 4.6 %collective-permute-start.1 = (f32[8,32,384]{2,1,0:T(8,128)S(1)}, f32[8,32,384]{2,1,0:T(8,128)S(1)}, u32[]{:S(2)}, u32[]{:S(2)}) collective-permute-start(f32[8,32,384]{2,1,0:T(8,128)S(1)} %collective-permute-done), channel_id=1, source_target_pairs={{0,8},{1,9},{2,10},{3,11},{4,12},{5,13},{6,14},{7,15},{8,0},{9,1},... | collective-permute-start | bytes 1179656 | tf_op jit(solution)/shard_map/ppermute | solution.py:173
  19.6 36.2 %copy-start.14 = (f32[16,32,384]{2,1,0:T(8,128)}, f32[16,32,384]{2,1,0:T(8,128)S(1)}, u32[]{:S(2)}) copy-start(f32[16,32,384]{2,1,0:T(8,128)S(1)} %get-tuple-element.17) | copy-start | bytes 2359300
  19.6 36.2 %copy-start.17 = (f32[16,32,384]{2,1,0:T(8,128)}, f32[16,32,384]{2,1,0:T(8,128)S(1)}, u32[]{:S(2)}) copy-start(f32[16,32,384]{2,1,0:T(8,128)S(1)} %get-tuple-element.18) | copy-start | bytes 2359300
  19.7 35.2 %collective-permute-start.3 = (f32[32,8,384]{2,1,0:T(8,128)S(1)}, f32[32,8,384]{2,1,0:T(8,128)S(1)}, u32[]{:S(2)}, u32[]{:S(2)}) collective-permute-start(f32[32,8,384]{2,1,0:T(8,128)S(1)} %get-tuple-element.52), channel_id=1, source_target_pairs={{0,1},{1,17},{2,3},{3,19},{4,5},{5,21},{6,7},{7,23},{8,9},{9,25},{... | collective-permute-start | bytes 1179656 | tf_op jit(solution)/shard_map/ppermute | solution.py:173
  22.9 33.0 %collective-permute-start.4 = (f32[32,8,384]{2,1,0:T(8,128)S(1)}, f32[32,8,384]{2,1,0:T(8,128)S(1)}, u32[]{:S(2)}, u32[]{:S(2)}) collective-permute-start(f32[32,8,384]{2,1,0:T(8,128)S(1)} %get-tuple-element.53), channel_id=1, source_target_pairs={{1,0},{3,2},{5,4},{7,6},{9,8},{11,10},{13,12},{15,14},{16,17},{17,... | collective-permute-start | bytes 1179656 | tf_op jit(solution)/shard_map/ppermute | solution.py:173
  54.9 2.2 copy-start.20
  55.8 1.2 copy-start.22
  57.1 15.3 %collective-permute-start.5 = (f32[8,48,384]{2,1,0:T(8,128)}, f32[8,48,384]{2,1,0:T(8,128)}, u32[]{:S(2)}, u32[]{:S(2)}) collective-permute-start(f32[8,48,384]{2,1,0:T(8,128)} %get-tuple-element.26), channel_id=1, source_target_pairs={{0,2},{1,3},{2,4},{3,5},{4,6},{5,7},{8,10},{9,11},{10,12},{11,13},... | collective-permute-start | bytes 1769480 | tf_op jit(solution)/shard_map/ppermute | solution.py:173
  60.3 15.0 %collective-permute-start.6 = (f32[8,48,384]{2,1,0:T(8,128)}, f32[8,48,384]{2,1,0:T(8,128)}, u32[]{:S(2)}, u32[]{:S(2)}) collective-permute-start(f32[8,48,384]{2,1,0:T(8,128)} %get-tuple-element.27), channel_id=1, source_target_pairs={{2,0},{3,1},{4,2},{5,3},{6,4},{7,5},{10,8},{11,9},{12,10},{13,11},... | collective-permute-start | bytes 1769480 | tf_op jit(solution)/shard_map/ppermute | solution.py:173
  67.7 7.6 %copy-start.15 = (f32[16,32,384]{2,1,0:T(8,128)S(1)}, f32[16,32,384]{2,1,0:T(8,128)}, u32[]{:S(2)}) copy-start(f32[16,32,384]{2,1,0:T(8,128)} %copy-done.14) | copy-start | bytes 2359300
  67.7 7.6 %copy-start.18 = (f32[16,32,384]{2,1,0:T(8,128)S(1)}, f32[16,32,384]{2,1,0:T(8,128)}, u32[]{:S(2)}) copy-start(f32[16,32,384]{2,1,0:T(8,128)} %copy-done.17) | copy-start | bytes 2359300
  67.7 7.6 %copy-start.21 = (f32[32,8,384]{2,1,0:T(8,128)S(1)}, f32[32,8,384]{2,1,0:T(8,128)}, u32[]{:S(2)}) copy-start(f32[32,8,384]{2,1,0:T(8,128)} %copy-done.20) | copy-start | bytes 1179652
  67.7 7.6 %copy-start.23 = (f32[32,8,384]{2,1,0:T(8,128)S(1)}, f32[32,8,384]{2,1,0:T(8,128)}, u32[]{:S(2)}) copy-start(f32[32,8,384]{2,1,0:T(8,128)} %copy-done.22) | copy-start | bytes 1179652
  67.9 8.8 %copy-start = (f32[32,32,384]{2,1,0:T(8,128)}, f32[32,32,384]{2,1,0:T(8,128)S(1)}, u32[]{:S(2)}) copy-start(f32[32,32,384]{2,1,0:T(8,128)S(1)} %get-tuple-element.75.d_ref) | copy-start | bytes 4718596
  68.0 8.8 %copy-start.2 = (f32[384,384]{0,1:T(8,128)S(1)}, f32[384,384]{0,1:T(8,128)}, u32[]{:S(2)}) copy-start(f32[384,384]{0,1:T(8,128)} %copy.14) | copy-start | bytes 1769476
  68.0 8.8 %copy-start.8 = (f32[128,192]{1,0:T(8,128)S(1)}, f32[128,192]{1,0:T(8,128)}, u32[]{:S(2)}) copy-start(f32[128,192]{1,0:T(8,128)} %mul.135.ax_ref) | copy-start | bytes 294916
  84.7 18.6 %collective-permute-start.15 = (f32[8,32,384]{2,1,0:T(8,128)S(1)}, f32[8,32,384]{2,1,0:T(8,128)S(1)}, u32[]{:S(2)}, u32[]{:S(2)}) collective-permute-start(f32[8,32,384]{2,1,0:T(8,128)S(1)} %get-tuple-element.46), channel_id=1, source_target_pairs={{2,0},{3,1},{4,2},{5,3},{6,4},{7,5},{10,8},{11,9},{12,10},{13,11},... | collective-permute-start | bytes 1179656 | tf_op jit(solution)/shard_map/ppermute | solution.py:173
  86.8 16.5 %collective-permute-start.14 = (f32[8,32,384]{2,1,0:T(8,128)S(1)}, f32[8,32,384]{2,1,0:T(8,128)S(1)}, u32[]{:S(2)}, u32[]{:S(2)}) collective-permute-start(f32[8,32,384]{2,1,0:T(8,128)S(1)} %get-tuple-element.47), channel_id=1, source_target_pairs={{0,2},{1,3},{2,4},{3,5},{4,6},{5,7},{8,10},{9,11},{10,12},{11,13},... | collective-permute-start | bytes 1179656 | tf_op jit(solution)/shard_map/ppermute | solution.py:173
  98.0 16.2 %collective-permute-start.11 = (f32[8,32,384]{2,1,0:T(8,128)S(1)}, f32[8,32,384]{2,1,0:T(8,128)S(1)}, u32[]{:S(2)}, u32[]{:S(2)}) collective-permute-start(f32[8,32,384]{2,1,0:T(8,128)S(1)} %get-tuple-element.50), channel_id=1, source_target_pairs={{2,0},{3,1},{4,2},{5,3},{6,4},{7,5},{10,8},{11,9},{12,10},{13,11},... | collective-permute-start | bytes 1179656 | tf_op jit(solution)/shard_map/ppermute | solution.py:173
  100.0 14.2 %collective-permute-start.10 = (f32[8,32,384]{2,1,0:T(8,128)S(1)}, f32[8,32,384]{2,1,0:T(8,128)S(1)}, u32[]{:S(2)}, u32[]{:S(2)}) collective-permute-start(f32[8,32,384]{2,1,0:T(8,128)S(1)} %get-tuple-element.51), channel_id=1, source_target_pairs={{0,2},{1,3},{2,4},{3,5},{4,6},{5,7},{8,10},{9,11},{10,12},{11,13},... | collective-permute-start | bytes 1179656 | tf_op jit(solution)/shard_map/ppermute | solution.py:173
  107.0 1.1 copy-start.4
  108.1 20.4 %collective-permute-start.17 = (f32[32,8,384]{2,1,0:T(8,128)}, f32[32,8,384]{2,1,0:T(8,128)}, u32[]{:S(2)}, u32[]{:S(2)}) collective-permute-start(f32[32,8,384]{2,1,0:T(8,128)} %get-tuple-element.44), channel_id=1, source_target_pairs={{1,0},{3,2},{5,4},{7,6},{9,8},{11,10},{13,12},{15,14},{16,17},{17,... | collective-permute-start | bytes 1179656 | tf_op jit(solution)/shard_map/ppermute | solution.py:173
  109.4 19.1 %collective-permute-start.16 = (f32[32,8,384]{2,1,0:T(8,128)}, f32[32,8,384]{2,1,0:T(8,128)}, u32[]{:S(2)}, u32[]{:S(2)}) collective-permute-start(f32[32,8,384]{2,1,0:T(8,128)} %get-tuple-element.45), channel_id=1, source_target_pairs={{0,1},{1,17},{2,3},{3,19},{4,5},{5,21},{6,7},{7,23},{8,9},{9,25},{... | collective-permute-start | bytes 1179656 | tf_op jit(solution)/shard_map/ppermute | solution.py:173
  117.8 1.1 copy-start.6
  118.9 17.7 %collective-permute-start.13 = (f32[32,8,384]{2,1,0:T(8,128)}, f32[32,8,384]{2,1,0:T(8,128)}, u32[]{:S(2)}, u32[]{:S(2)}) collective-permute-start(f32[32,8,384]{2,1,0:T(8,128)} %get-tuple-element.48), channel_id=1, source_target_pairs={{1,0},{3,2},{5,4},{7,6},{9,8},{11,10},{13,12},{15,14},{16,17},{17,... | collective-permute-start | bytes 1179656 | tf_op jit(solution)/shard_map/ppermute | solution.py:173
  120.2 16.5 %collective-permute-start.12 = (f32[32,8,384]{2,1,0:T(8,128)}, f32[32,8,384]{2,1,0:T(8,128)}, u32[]{:S(2)}, u32[]{:S(2)}) collective-permute-start(f32[32,8,384]{2,1,0:T(8,128)} %get-tuple-element.49), channel_id=1, source_target_pairs={{0,1},{1,17},{2,3},{3,19},{4,5},{5,21},{6,7},{7,23},{8,9},{9,25},{... | collective-permute-start | bytes 1179656 | tf_op jit(solution)/shard_map/ppermute | solution.py:173
  128.5 1.4 copy-start.5
  129.9 0.9 copy-start.11
  130.8 5.9 %copy-start.7 = (f32[32,32,384]{2,1,0:T(8,128)S(1)}, f32[32,32,384]{2,1,0:T(8,128)}, u32[]{:S(2)}) copy-start(f32[32,32,384]{2,1,0:T(8,128)} %copy-done.6) | copy-start | bytes 4718596
  130.8 5.9 %copy-start.10 = (f32[128,192]{1,0:T(8,128)S(1)}, f32[128,192]{1,0:T(8,128)}, u32[]{:S(2)}) copy-start(f32[128,192]{1,0:T(8,128)} %mul.132.ax_ref) | copy-start | bytes 294916
  136.7 14.2 %copy-start.16 = (f32[16,32,384]{2,1,0:T(8,128)S(1)}, f32[16,32,384]{2,1,0:T(8,128)}, u32[]{:S(2)}) copy-start(f32[16,32,384]{2,1,0:T(8,128)} %copy-done.14) | copy-start | bytes 2359300
  136.7 14.2 %copy-start.19 = (f32[16,32,384]{2,1,0:T(8,128)S(1)}, f32[16,32,384]{2,1,0:T(8,128)}, u32[]{:S(2)}) copy-start(f32[16,32,384]{2,1,0:T(8,128)} %copy-done.17) | copy-start | bytes 2359300
  142.6 8.3 %collective-permute-start.18 = (f32[32,32,384]{2,1,0:T(8,128)S(1)}, f32[32,32,384]{2,1,0:T(8,128)S(1)}, u32[]{:S(2)}, u32[]{:S(2)}) collective-permute-start(f32[32,32,384]{2,1,0:T(8,128)S(1)} %shard_map.51), channel_id=1, source_target_pairs={{0,8},{1,9},{2,10},{3,11},{4,12},{5,13},{6,14},{7,15},{8,0},{9,1},... | collective-permute-start | bytes 4718600 | tf_op jit(solution)/shard_map/ppermute | solution.py:173
  151.7 31.9 %copy-start.13 = (f32[32,32,384]{2,1,0:T(8,128)}, f32[32,32,384]{2,1,0:T(8,128)S(1)}, u32[]{:S(2)}) copy-start(f32[32,32,384]{2,1,0:T(8,128)S(1)} %fusion) | copy-start | bytes 4718596
  151.8 10.1 %collective-permute-start.19 = (f32[32,8,384]{2,1,0:T(8,128)S(1)}, f32[32,8,384]{2,1,0:T(8,128)S(1)}, u32[]{:S(2)}, u32[]{:S(2)}) collective-permute-start(f32[32,8,384]{2,1,0:T(8,128)S(1)} %get-tuple-element.42), channel_id=1, source_target_pairs={{0,1},{1,17},{2,3},{3,19},{4,5},{5,21},{6,7},{7,23},{8,9},{9,25},{... | collective-permute-start | bytes 1179656 | tf_op jit(solution)/shard_map/ppermute | solution.py:173
  153.8 12.2 %collective-permute-start.20 = (f32[32,8,384]{2,1,0:T(8,128)S(1)}, f32[32,8,384]{2,1,0:T(8,128)S(1)}, u32[]{:S(2)}, u32[]{:S(2)}) collective-permute-start(f32[32,8,384]{2,1,0:T(8,128)S(1)} %get-tuple-element.43), channel_id=1, source_target_pairs={{1,0},{3,2},{5,4},{7,6},{9,8},{11,10},{13,12},{15,14},{16,17},{17,... | collective-permute-start | bytes 1179656 | tf_op jit(solution)/shard_map/ppermute | solution.py:173
  166.1 15.4 %collective-permute-start.21 = (f32[8,48,384]{2,1,0:T(8,128)S(1)}, f32[8,48,384]{2,1,0:T(8,128)S(1)}, u32[]{:S(2)}, u32[]{:S(2)}) collective-permute-start(f32[8,48,384]{2,1,0:T(8,128)S(1)} %get-tuple-element.24), channel_id=1, source_target_pairs={{0,2},{1,3},{2,4},{3,5},{4,6},{5,7},{8,10},{9,11},{10,12},{11,13},... | collective-permute-start | bytes 1769480 | tf_op jit(solution)/shard_map/ppermute | solution.py:173
  168.0 15.9 %copy-start.1 = (f32[32,32,384]{2,1,0:T(8,128)S(1)}, f32[32,32,384]{2,1,0:T(8,128)}, u32[]{:S(2)}) copy-start(f32[32,32,384]{2,1,0:T(8,128)} %copy-done) | copy-start | bytes 4718596
  168.0 15.9 %copy-start.3 = (f32[384,384]{0,1:T(8,128)S(1)}, f32[384,384]{0,1:T(8,128)}, u32[]{:S(2)}) copy-start(f32[384,384]{0,1:T(8,128)} %copy.14) | copy-start | bytes 1769476
  168.0 15.9 %copy-start.9 = (f32[128,192]{1,0:T(8,128)S(1)}, f32[128,192]{1,0:T(8,128)}, u32[]{:S(2)}) copy-start(f32[128,192]{1,0:T(8,128)} %mul.135.ax_ref) | copy-start | bytes 294916
  168.0 15.6 %collective-permute-start.22 = (f32[8,48,384]{2,1,0:T(8,128)S(1)}, f32[8,48,384]{2,1,0:T(8,128)S(1)}, u32[]{:S(2)}, u32[]{:S(2)}) collective-permute-start(f32[8,48,384]{2,1,0:T(8,128)S(1)} %get-tuple-element.25), channel_id=1, source_target_pairs={{2,0},{3,1},{4,2},{5,3},{6,4},{7,5},{10,8},{11,9},{12,10},{13,11},... | collective-permute-start | bytes 1769480 | tf_op jit(solution)/shard_map/ppermute | solution.py:173
  191.8 18.6 %collective-permute-start.28 = (f32[8,32,384]{2,1,0:T(8,128)S(1)}, f32[8,32,384]{2,1,0:T(8,128)S(1)}, u32[]{:S(2)}, u32[]{:S(2)}) collective-permute-start(f32[8,32,384]{2,1,0:T(8,128)S(1)} %get-tuple-element.36), channel_id=1, source_target_pairs={{2,0},{3,1},{4,2},{5,3},{6,4},{7,5},{10,8},{11,9},{12,10},{13,11},... | collective-permute-start | bytes 1179656 | tf_op jit(solution)/shard_map/ppermute | solution.py:173
  194.9 15.5 %collective-permute-start.27 = (f32[8,32,384]{2,1,0:T(8,128)S(1)}, f32[8,32,384]{2,1,0:T(8,128)S(1)}, u32[]{:S(2)}, u32[]{:S(2)}) collective-permute-start(f32[8,32,384]{2,1,0:T(8,128)S(1)} %get-tuple-element.37), channel_id=1, source_target_pairs={{0,2},{1,3},{2,4},{3,5},{4,6},{5,7},{8,10},{9,11},{10,12},{11,13},... | collective-permute-start | bytes 1179656 | tf_op jit(solution)/shard_map/ppermute | solution.py:173
  205.0 13.4 %collective-permute-start.24 = (f32[8,32,384]{2,1,0:T(8,128)S(1)}, f32[8,32,384]{2,1,0:T(8,128)S(1)}, u32[]{:S(2)}, u32[]{:S(2)}) collective-permute-start(f32[8,32,384]{2,1,0:T(8,128)S(1)} %get-tuple-element.40), channel_id=1, source_target_pairs={{2,0},{3,1},{4,2},{5,3},{6,4},{7,5},{10,8},{11,9},{12,10},{13,11},... | collective-permute-start | bytes 1179656 | tf_op jit(solution)/shard_map/ppermute | solution.py:173
  208.1 10.4 %collective-permute-start.23 = (f32[8,32,384]{2,1,0:T(8,128)S(1)}, f32[8,32,384]{2,1,0:T(8,128)S(1)}, u32[]{:S(2)}, u32[]{:S(2)}) collective-permute-start(f32[8,32,384]{2,1,0:T(8,128)S(1)} %get-tuple-element.41), channel_id=1, source_target_pairs={{0,2},{1,3},{2,4},{3,5},{4,6},{5,7},{8,10},{9,11},{10,12},{11,13},... | collective-permute-start | bytes 1179656 | tf_op jit(solution)/shard_map/ppermute | solution.py:173
  213.1 13.4 %collective-permute-start.30 = (f32[32,8,384]{2,1,0:T(8,128)S(1)}, f32[32,8,384]{2,1,0:T(8,128)S(1)}, u32[]{:S(2)}, u32[]{:S(2)}) collective-permute-start(f32[32,8,384]{2,1,0:T(8,128)S(1)} %get-tuple-element.34), channel_id=1, source_target_pairs={{1,0},{3,2},{5,4},{7,6},{9,8},{11,10},{13,12},{15,14},{16,17},{17,... | collective-permute-start | bytes 1179656 | tf_op jit(solution)/shard_map/ppermute | solution.py:173
  214.4 12.1 %collective-permute-start.29 = (f32[32,8,384]{2,1,0:T(8,128)S(1)}, f32[32,8,384]{2,1,0:T(8,128)S(1)}, u32[]{:S(2)}, u32[]{:S(2)}) collective-permute-start(f32[32,8,384]{2,1,0:T(8,128)S(1)} %get-tuple-element.35), channel_id=1, source_target_pairs={{0,1},{1,17},{2,3},{3,19},{4,5},{5,21},{6,7},{7,23},{8,9},{9,25},{... | collective-permute-start | bytes 1179656 | tf_op jit(solution)/shard_map/ppermute | solution.py:173
  221.1 5.4 %copy-start.12 = (f32[128,192]{1,0:T(8,128)S(1)}, f32[128,192]{1,0:T(8,128)}, u32[]{:S(2)}) copy-start(f32[128,192]{1,0:T(8,128)} %mul.138.ax_ref) | copy-start | bytes 294916
  221.2 9.9 %collective-permute-start.26 = (f32[32,8,384]{2,1,0:T(8,128)S(1)}, f32[32,8,384]{2,1,0:T(8,128)S(1)}, u32[]{:S(2)}, u32[]{:S(2)}) collective-permute-start(f32[32,8,384]{2,1,0:T(8,128)S(1)} %get-tuple-element.38), channel_id=1, source_target_pairs={{1,0},{3,2},{5,4},{7,6},{9,8},{11,10},{13,12},{15,14},{16,17},{17,... | collective-permute-start | bytes 1179656 | tf_op jit(solution)/shard_map/ppermute | solution.py:173
  222.5 9.0 %collective-permute-start.25 = (f32[32,8,384]{2,1,0:T(8,128)S(1)}, f32[32,8,384]{2,1,0:T(8,128)S(1)}, u32[]{:S(2)}, u32[]{:S(2)}) collective-permute-start(f32[32,8,384]{2,1,0:T(8,128)S(1)} %get-tuple-element.39), channel_id=1, source_target_pairs={{0,1},{1,17},{2,3},{3,19},{4,5},{5,21},{6,7},{7,23},{8,9},{9,25},{... | collective-permute-start | bytes 1179656 | tf_op jit(solution)/shard_map/ppermute | solution.py:173
  236.1 7.9 %collective-permute-start.31 = (f32[32,32,384]{2,1,0:T(8,128)S(1)}, f32[32,32,384]{2,1,0:T(8,128)}, u32[]{:S(2)}, u32[]{:S(2)}) collective-permute-start(f32[32,32,384]{2,1,0:T(8,128)S(1)} %shard_map.57), channel_id=1, source_target_pairs={{0,8},{1,9},{2,10},{3,11},{4,12},{5,13},{6,14},{7,15},{8,0},{9,1},... | collective-permute-start | bytes 4718600 | tf_op jit(solution)/shard_map/ppermute | solution.py:173
  246.8 12.4 %collective-permute-start.34 = (f32[8,32,384]{2,1,0:T(8,128)S(1)}, f32[8,32,384]{2,1,0:T(8,128)S(1)}, u32[]{:S(2)}, u32[]{:S(2)}) collective-permute-start(f32[8,32,384]{2,1,0:T(8,128)S(1)} %get-tuple-element.32), channel_id=1, source_target_pairs={{0,17},{1,16},{2,19},{3,18},{4,21},{5,20},{6,23},{7,22},{8,25},{9,... | collective-permute-start | bytes 1179656 | tf_op jit(solution)/shard_map/ppermute | solution.py:173
  250.1 18.0 %collective-permute-start.32 = (f32[8,32,384]{2,1,0:T(8,128)S(1)}, f32[8,32,384]{2,1,0:T(8,128)S(1)}, u32[]{:S(2)}, u32[]{:S(2)}) collective-permute-start(f32[8,32,384]{2,1,0:T(8,128)S(1)} %get-tuple-element.32), channel_id=1, source_target_pairs={{0,1},{1,0},{2,3},{3,2},{4,5},{5,4},{6,7},{7,6},{8,9},{9,8},{10,11... | collective-permute-start | bytes 1179656 | tf_op jit(solution)/shard_map/ppermute | solution.py:173
  250.5 17.6 %collective-permute-start.33 = (f32[8,32,384]{2,1,0:T(8,128)S(1)}, f32[8,32,384]{2,1,0:T(8,128)S(1)}, u32[]{:S(2)}, u32[]{:S(2)}) collective-permute-start(f32[8,32,384]{2,1,0:T(8,128)S(1)} %get-tuple-element.33), channel_id=1, source_target_pairs={{0,16},{1,17},{2,18},{3,19},{4,20},{5,21},{6,22},{7,23},{8,24},{9,... | collective-permute-start | bytes 1179656 | tf_op jit(solution)/shard_map/ppermute | solution.py:173
  268.4 3.8 %collective-permute-start.35 = (f32[8,128,384]{2,1,0:T(8,128)S(1)}, f32[8,128,384]{2,1,0:T(8,128)S(1)}, u32[]{:S(2)}, u32[]{:S(2)}) collective-permute-start(f32[8,128,384]{2,1,0:T(8,128)S(1)} %pad_maximum_fusion.6), channel_id=1, source_target_pairs={{0,8},{1,9},{2,10},{3,11},{4,12},{5,13},{6,14},{7,15},{8,0},{9,1},... | collective-permute-start | bytes 4718600 | tf_op jit(solution)/shard_map/ppermute | solution.py:173
where the time goes:
time: 278 us; the launch traced here: 274 us
  waiting for transfers between devices  91.1 us (33%)
  starting transfers between devices  85.1 us (31%)
  Pallas kernels  62.9 us (23%)
  local copies, waits for them, and re-layouts  17.2 us (6%)
  other arithmetic  16.7 us (6%)
    ppermute x36, waiting for transfers between devices, move(): return lax.ppermute(value, AXES, pairs)  91.1 us
    ppermute x36, starting transfers between devices, move(): return lax.ppermute(value, AXES, pairs)  85.1 us
    pallas_call x4, Pallas kernels, blur_forward(): pl.pallas_call(forward_kernel, out_shape=jax.ShapeDtypeStruct(data.shape,...  31.4 us
    pallas_call x4, Pallas kernels, blur_back(): pl.pallas_call(back_kernel, out_shape=jax.ShapeDtypeStruct(u.shape, jnp.f...  20.8 us
    pallas_call x4, Pallas kernels, smear(): pl.pallas_call(smear_kernel, grid=(rows // 8,), out_shape=jax.ShapeDtypeS...  10.7 us
  transfers between devices with their start and end apart: 36, of which 16 were waited for; matrix products, arithmetic and copies ran while one was open for 7% of the time, Pallas kernels for 13%

commit v1 on v0

v1 whole, which is shorter than its diff:
```python
import functools
import jax
import jax.numpy as jnp
from jax import lax
from jax.experimental import pallas as pl
from jax.experimental.pallas import tpu as pltpu
from jax.sharding import PartitionSpec as P

ITERS = 2
GROUP = 8
PLANES = 4
MESH = pl.DeviceIdType.MESH
VMEM = pl.BlockSpec(memory_space=pltpu.VMEM)
ANY = pl.BlockSpec(memory_space=pl.ANY)
MIB = 1024 * 1024


def split(value):
    high = value.astype(jnp.bfloat16)
    return high, (value - high.astype(jnp.float32)).astype(jnp.bfloat16)


def dot(lhs, rhs):
    return jnp.dot(lhs, rhs, preferred_element_type=jnp.float32)


def odd_stride(rows):
    return rows + 8 if (rows // 8) % 2 == 0 else rows


class Place:
    def __init__(self, blocks):
        view, gz = lax.axis_index("view"), lax.axis_index("gz")
        self.blocks = blocks
        self.a, self.c = view // 2, view % 2
        self.k, self.b = gz // 2, gz % 2
        self.strip = self.strip_of(self.a, self.b)

    @staticmethod
    def strip_of(a, b):
        return 2 * a + (a + b) % 2

    def device(self, a=None, c=None, k=None, b=None):
        a = self.a if a is None else a
        c = self.c if c is None else c
        k = self.k if k is None else k
        b = self.b if b is None else b
        return (2 * a + c, 2 * k + b)

    def of_strip(self, strip):
        return self.device(a=strip // 2, b=(strip % 2 + strip // 2) % 2)

    def partner(self):
        return self.device(c=1 - self.c)

    def others(self):
        a, b = self.a, self.b
        return ((a, 1 - b), (1 - a, b), (1 - a, 1 - b))


def remote(src, dst, sems, index, device):
    send, recv = sems
    return pltpu.make_async_remote_copy(
        src_ref=src, dst_ref=dst, send_sem=send.at[index], recv_sem=recv.at[index],
        device_id=device, device_id_type=MESH,
    )


def greet(here, along_z, along_strips, square):
    barrier = pltpu.get_barrier_semaphore()

    def signal(device):
        pl.semaphore_signal(barrier, inc=1, device_id=device, device_id_type=MESH)

    signal(here.partner())
    count = 1
    if square:
        for a, b in here.others():
            signal(here.device(a=a, b=b))
        count += 3
    around = []
    if along_z:
        around += [(here.k + step, here.blocks, lambda to: here.device(k=to)) for step in (-1, 1)]
    if along_strips:
        around += [(here.strip + step, 4, here.of_strip) for step in (-1, 1)]
    for there, limit, device in around:
        inside = (there >= 0) & (there < limit)
        pl.when(inside)(functools.partial(lambda there, device: signal(device(there)), there, device))
        count = count + inside.astype(jnp.int32)
    pl.semaphore_wait(barrier, count)


def band(taps, outputs, inputs, sign, shift):
    at = sign * (
        lax.broadcasted_iota(jnp.int32, (outputs, inputs), 1)
        - lax.broadcasted_iota(jnp.int32, (outputs, inputs), 0)
    ) + shift
    total = jnp.zeros((outputs, inputs), jnp.float32)
    for tap, value in enumerate(taps):
        total = jnp.where(at == tap, value, total)
    return total


def write_left(ref, index, matrix):
    high, low = split(matrix)
    rows, depth = matrix.shape
    top = jnp.concatenate([high, high], axis=1)
    bottom = jnp.concatenate([low, low], axis=1)
    ref[index] = jnp.concatenate([top, bottom], axis=0)


def write_right(ref, index, matrix):
    high, low = split(matrix)
    half = jnp.concatenate([high, low], axis=1)
    ref[index] = jnp.concatenate([half, half], axis=0)


def write_matrices(kern_ref, taps, refs):
    lz_ref, x_ref, ly_ref, lyb_ref, xb_ref, lzb_ref = refs
    reach = taps - 1
    pad = reach // 2
    for which in range(2):
        rows = kern_ref[which]
        kz, kx, ky = ([rows[r:r + 1, t:t + 1] for t in range(taps)] for r in range(3))
        outputs, inputs = lz_ref.shape[1] // 2, lz_ref.shape[2] // 2
        write_left(lz_ref, which, band(kz, outputs, inputs, 1, 0))
        write_right(x_ref, which, band(kx, x_ref.shape[1] // 2, x_ref.shape[2] // 2, -1, pad))
        write_left(ly_ref, which, band(ky, ly_ref.shape[1] // 2, ly_ref.shape[2] // 2, 1, 0))
        write_left(lyb_ref, which, band(ky, lyb_ref.shape[1] // 2, lyb_ref.shape[2] // 2, -1, reach))
        write_right(xb_ref, which, band(kx, xb_ref.shape[1] // 2, xb_ref.shape[2] // 2, 1, pad))
        write_left(lzb_ref, which, band(kz, lzb_ref.shape[1] // 2, lzb_ref.shape[2] // 2, -1, reach))


def setup_kernel(blocks, taps, strip_rows, data_hbm, start_hbm, kern_in,
                 est_ref, data_ref, lz_ref, x_ref, ly_ref, lyb_ref, xb_ref, lzb_ref,
                 sbuf, dbuf, ts_ref, td_ref, kern_ref,
                 load_sem, kern_s, kern_r, e_s, e_r, d_s, d_r, h_s, h_r):
    here = Place(blocks)
    planes, width_x, width_y = start_hbm.shape
    reach = taps - 1
    pad = reach // 2
    wide = strip_rows + 2 * reach
    tall = strip_rows + 2 * pad
    stride = ts_ref.shape[0] // (width_y + 2 * reach)
    half = wide // 2
    k, a, b, c = here.k, here.a, here.b, here.c
    load_start = pltpu.make_async_copy(start_hbm, sbuf, load_sem.at[0])
    load_data = pltpu.make_async_copy(data_hbm, dbuf, load_sem.at[1])
    load_start.start()
    load_data.start()
    ts3 = ts_ref.reshape(width_y + 2 * reach, stride, width_x)
    greet(here, True, False, True)

    kern_ref[a] = kern_in[...]
    kern_copy = remote(kern_in, kern_ref.at[a], (kern_s, kern_r), 0, here.device(a=1 - a))
    kern_copy.start()

    ts_ref[pl.ds(0, reach * stride)] = jnp.zeros((reach * stride, width_x), jnp.float32)
    ts_ref[pl.ds((width_y + reach) * stride, reach * stride)] = jnp.zeros((reach * stride, width_x), jnp.float32)
    load_start.wait()

    @pl.loop(0, planes)
    def _(z):
        ts_ref[pl.ds(reach * stride + z, width_y, stride=stride)] = sbuf[z].T

    mine = pl.multiple_of(reach + planes * b, planes)
    theirs = pl.multiple_of(reach + planes * (1 - b), planes)
    rows = pl.ds(half * c, half)
    to_strip = here.strip_of(a, 1 - b)
    e_copy = remote(
        ts3.at[pl.ds(strip_rows * to_strip + half * c, half), pl.ds(0, planes)],
        est_ref.at[rows, pl.ds(mine, planes)], (e_s, e_r), 0, here.device(b=1 - b),
    )
    e_copy.start()

    for z in range(planes):
        td_ref[z, pl.ds(0, pad)] = jnp.zeros((pad, width_x), jnp.float32)
        td_ref[z, pl.ds(pad + width_y, pad)] = jnp.zeros((pad, width_x), jnp.float32)
    load_data.wait()

    @pl.loop(0, planes)
    def _(z):
        td_ref[z, pl.ds(pad, width_y)] = dbuf[z].T

    edge = (b * (planes - pad), pad)
    inner = ((1 - b) * pad, planes - pad)
    d_copies = []
    for part, (first, size) in enumerate((edge, inner)):
        for kind, (oa, ob) in enumerate(here.others()):
            copy = remote(
                td_ref.at[pl.ds(first, size), pl.ds(strip_rows * here.strip_of(oa, ob), tall)],
                data_ref.at[a, pl.ds(pad + planes * b + first, size)],
                (d_s, d_r), 3 * part + kind, here.device(a=oa, b=ob),
            )
            copy.start()
            d_copies.append(copy)

    @pl.loop(0, wide)
    def _(row):
        est_ref[row, pl.ds(mine, planes)] = ts3[strip_rows * here.strip + row, pl.ds(0, planes)]

    @pl.loop(0, planes)
    def _(z):
        data_ref[a, pad + planes * b + z] = td_ref[z, pl.ds(pl.multiple_of(strip_rows * here.strip, 8), tall)]

    below, above = k > 0, k < blocks - 1

    def zero_est(first):
        @pl.loop(0, wide)
        def _(row):
            est_ref[row, pl.ds(first, reach)] = jnp.zeros((reach, width_x), jnp.float32)

    pl.when(jnp.logical_not(below))(lambda: zero_est(0))
    pl.when(jnp.logical_not(above))(lambda: zero_est(reach + 2 * planes))

    def halo(kind, oa, ob):
        to = k + 2 * ob - 1
        source = k + 1 - 2 * ob
        place = (1 - ob) * (2 * planes + pad)
        copy = remote(
            data_ref.at[oa, pl.ds(pad + ob * (2 * planes - pad), pad)],
            data_ref.at[oa, pl.ds(place, pad)],
            (h_s, h_r), kind, here.device(k=to),
        )
        sends = (to >= 0) & (to < blocks)
        gets = (source >= 0) & (source < blocks)

        @pl.when(jnp.logical_not(gets))
        def _():
            @pl.loop(0, pad)
            def _(z):
                data_ref[oa, place + z] = jnp.zeros((tall, width_x), jnp.float32)

        pl.when(sends)(copy.start)
        return copy, sends, gets

    halos = [halo(3, a, b)]

    kern_copy.wait()
    write_matrices(kern_ref, taps, (lz_ref, x_ref, ly_ref, lyb_ref, xb_ref, lzb_ref))

    e_copy.wait()
    relay = remote(
        est_ref.at[rows, pl.ds(theirs, planes)], est_ref.at[rows, pl.ds(theirs, planes)],
        (e_s, e_r), 1, here.partner(),
    )
    up = remote(
        est_ref.at[rows, pl.ds(2 * planes, reach)], est_ref.at[rows, pl.ds(0, reach)],
        (e_s, e_r), 2, here.device(k=k + 1),
    )
    down = remote(
        est_ref.at[rows, pl.ds(reach, reach)], est_ref.at[rows, pl.ds(reach + 2 * planes, reach)],
        (e_s, e_r), 3, here.device(k=k - 1),
    )
    pl.when(above)(up.start)
    pl.when(below)(down.start)
    relay.start()
    from_below = remote(
        est_ref.at[rows, pl.ds(0, reach)], est_ref.at[rows, pl.ds(0, reach)],
        (e_s, e_r), 4, here.partner(),
    )
    from_above = remote(
        est_ref.at[rows, pl.ds(reach + 2 * planes, reach)], est_ref.at[rows, pl.ds(reach + 2 * planes, reach)],
        (e_s, e_r), 5, here.partner(),
    )

    @pl.when(below)
    def _():
        up.wait_recv()
        from_below.start()

    @pl.when(above)
    def _():
        down.wait_recv()
        from_above.start()

    for kind, (oa, ob) in enumerate(here.others()):
        d_copies[kind].wait_recv()
        halos.append(halo(kind, oa, ob))

    pl.when(above)(up.wait_send)
    pl.when(below)(down.wait_send)
    relay.wait()
    pl.when(below)(from_below.wait)
    pl.when(above)(from_above.wait)
    for copy in d_copies[3:]:
        copy.wait_recv()
    for copy in d_copies:
        copy.wait_send()
    for copy, sends, gets in halos:
        pl.when(sends)(copy.wait_send)
        pl.when(gets)(copy.wait_recv)


def sides(product):
    half = product.shape[1] // 2
    return product[:, :half] + product[:, half:]


def stack(product):
    half = product.shape[0] // 2
    return product[:half] + product[half:]


def iteration_kernel(est_ref, data_ref, lz_ref, x_ref, ly_ref, lyb_ref, xb_ref, lzb_ref,
                     out_ref, t_ref, s_ref):
    wide, deep, lanes = est_ref.shape
    _, outer, tall, _ = data_ref.shape
    rows, planes, _ = out_ref.shape
    t_stride = t_ref.shape[1] // wide
    s_stride = s_ref.shape[1] // outer
    cut = lambda value, count: [value[:, i * lanes:(i + 1) * lanes] for i in range(count)]

    @pl.loop(0, wide // GROUP)
    def _(step):
        base = step * GROUP
        right = jnp.concatenate(
            [jnp.concatenate(split(est_ref[base + i]), axis=0) for i in range(GROUP)], axis=1
        )
        for which in range(2):
            along_z = stack(dot(lz_ref[which], right))
            left = jnp.concatenate(split(jnp.concatenate(cut(along_z, GROUP), axis=0)), axis=1)
            along_x = sides(dot(left, x_ref[which]))
            for i in range(GROUP):
                t_ref[which, pl.ds(pl.multiple_of((base + i) * t_stride, 8), outer)] = along_x[i * outer:(i + 1) * outer]

    @pl.loop(0, outer // PLANES)
    def _(step):
        base = step * PLANES
        for which in range(2):
            right = jnp.concatenate([
                jnp.concatenate(split(t_ref[which, pl.ds(base + i, wide, stride=t_stride)]), axis=0)
                for i in range(PLANES)
            ], axis=1)
            blurred = stack(dot(ly_ref[which], right))
            data = jnp.concatenate([data_ref[which, base + i] for i in range(PLANES)], axis=1)
            right = jnp.concatenate(split(data / blurred), axis=0)
            along_y = stack(dot(lyb_ref[which], right))
            left = jnp.concatenate(split(jnp.concatenate(cut(along_y, PLANES), axis=0)), axis=1)
            along_x = sides(dot(left, xb_ref[which]))
            for i in range(PLANES):
                s_ref[which, pl.ds(pl.multiple_of((base + i) * s_stride, 8), rows)] = along_x[i * rows:(i + 1) * rows]

    @pl.loop(0, rows // GROUP)
    def _(step):
        base = step * GROUP
        both = []
        for which in range(2):
            right = jnp.concatenate([
                jnp.concatenate(split(s_ref[which, pl.ds(base + i, outer, stride=s_stride)]), axis=0)
                for i in range(GROUP)
            ], axis=1)
            both.append(stack(dot(lzb_ref[which], right)))
        for i, piece in enumerate(cut(both[0] * both[1], GROUP)):
            out_ref[base + i] = piece


def root(value):
    return jnp.sqrt(jnp.sqrt(value))


def swap_and_update(here, product_ref, other_ref, sems, update, first):
    rows = product_ref.shape[0]
    chunks = 4
    size = rows // chunks
    copies = []
    for i in range(chunks):
        at = pl.ds(i * size, size)
        copy = remote(product_ref.at[at], other_ref.at[at], sems, first + i, here.partner())
        copy.start()
        copies.append(copy)
    for i in range(chunks):
        copies[i].wait_recv()

        @pl.loop(0, size)
        def _(row):
            update(i * size + row, root(product_ref[i * size + row] * other_ref[i * size + row]))
    return copies


def middle_kernel(blocks, product_ref, old_ref, est_ref, other_ref, p_s, p_r, y_s, y_r, z_s, z_r, q_s, q_r):
    here = Place(blocks)
    rows, depth, lanes = product_ref.shape
    wide, deep, _ = old_ref.shape
    reach = (wide - rows) // 2
    k, c, strip = here.k, here.c, here.strip
    below, above = k > 0, k < blocks - 1
    left, right = strip > 0, strip < 3
    inside = pl.ds(reach, depth)
    greet(here, True, True, False)

    def update(row, factor):
        est_ref[reach + row, inside] = old_ref[reach + row, inside] * factor

    product_copies = swap_and_update(here, product_ref, other_ref, (p_s, p_r), update, 0)

    to_left = remote(
        est_ref.at[pl.ds(reach, reach), inside], est_ref.at[pl.ds(reach + rows, reach), inside],
        (y_s, y_r), 0, here.of_strip(strip - 1),
    )
    to_right = remote(
        est_ref.at[pl.ds(rows, reach), inside], est_ref.at[pl.ds(0, reach), inside],
        (y_s, y_r), 1, here.of_strip(strip + 1),
    )
    pl.when(left)(to_left.start)
    pl.when(right)(to_right.start)

    def pair(at, index):
        up = remote(
            est_ref.at[at, pl.ds(depth, reach)], est_ref.at[at, pl.ds(0, reach)],
            (z_s, z_r), index, here.device(k=k + 1),
        )
        down = remote(
            est_ref.at[at, pl.ds(reach, reach)], est_ref.at[at, pl.ds(reach + depth, reach)],
            (z_s, z_r), index + 1, here.device(k=k - 1),
        )
        from_below = remote(
            est_ref.at[at, pl.ds(0, reach)], est_ref.at[at, pl.ds(0, reach)],
            (q_s, q_r), index, here.partner(),
        )
        from_above = remote(
            est_ref.at[at, pl.ds(reach + depth, reach)], est_ref.at[at, pl.ds(reach + depth, reach)],
            (q_s, q_r), index + 1, here.partner(),
        )
        return up, down, from_below, from_above

    main = pair(pl.ds(reach + c * (rows // 2), rows // 2), 0)
    pl.when(above)(main[0].start)
    pl.when(below)(main[1].start)

    def zero(first_row, count, first, size):
        @pl.loop(0, count)
        def _(row):
            est_ref[first_row + row, pl.ds(first, size)] = jnp.zeros((size, lanes), jnp.float32)

    pl.when(jnp.logical_not(left))(lambda: zero(0, reach, reach, depth))
    pl.when(jnp.logical_not(right))(lambda: zero(reach + rows, reach, reach, depth))
    pl.when(jnp.logical_not(below))(lambda: zero(0, wide, 0, reach))
    pl.when(jnp.logical_not(above))(lambda: zero(0, wide, reach + depth, reach))

    pl.when(left)(to_right.wait_recv)
    pl.when(right)(to_left.wait_recv)
    corner = pair(pl.ds(c * (reach + rows), reach), 2)
    pl.when(above)(corner[0].start)
    pl.when(below)(corner[1].start)

    for up, down, from_below, from_above in (main, corner):
        @pl.when(below)
        def _():
            up.wait_recv()
            from_below.start()

        @pl.when(above)
        def _():
            down.wait_recv()
            from_above.start()

    for copy in product_copies:
        copy.wait_send()
    pl.when(left)(to_left.wait_send)
    pl.when(right)(to_right.wait_send)
    for up, down, from_below, from_above in (main, corner):
        pl.when(above)(up.wait_send)
        pl.when(below)(down.wait_send)
        pl.when(below)(from_below.wait)
        pl.when(above)(from_above.wait)


def last_kernel(blocks, product_ref, old_ref, all_ref, other_ref, new_ref, p_s, p_r, g_s, g_r, q_s, q_r):
    here = Place(blocks)
    rows, depth, lanes = product_ref.shape
    wide = old_ref.shape[0]
    reach = (wide - rows) // 2
    planes = depth // 2
    a, b, c, strip = here.a, here.b, here.c, here.strip
    greet(here, False, False, True)

    def update(row, factor):
        new_ref[row] = old_ref[reach + row, pl.ds(reach, depth)] * factor

    product_copies = swap_and_update(here, product_ref, other_ref, (p_s, p_r), update, 0)
    half = rows // 2
    copies = []
    for kind, (oa, ob) in enumerate(here.others()):
        copy = remote(
            new_ref.at[pl.ds(half * c, half), pl.ds(pl.multiple_of(planes * ob, 8), planes)],
            all_ref.at[pl.ds(rows * strip + half * c, half), pl.ds(0, planes)],
            (g_s, g_r), kind, here.device(a=oa, b=ob),
        )
        copy.start()
        copies.append(copy)

    @pl.loop(0, rows)
    def _(row):
        all_ref[rows * strip + row, pl.ds(0, planes)] = new_ref[row, pl.ds(pl.multiple_of(planes * b, 8), planes)]

    relays = []
    for kind, (oa, ob) in enumerate(here.others()):
        copies[kind].wait_recv()
        at = pl.ds(rows * here.strip_of(oa, ob) + half * c, half)
        relay = remote(
            all_ref.at[at, pl.ds(0, planes)], all_ref.at[at, pl.ds(0, planes)],
            (q_s, q_r), kind, here.partner(),
        )
        relay.start()
        relays.append(relay)
    for copy in product_copies + copies:
        copy.wait_send()
    for relay in relays:
        relay.wait()


def output_kernel(all_ref, out_ref):
    group, lanes, width = out_ref.shape
    stride = all_ref.shape[0] // width
    base = pl.program_id(0) * group
    for i in range(group):
        out_ref[i] = all_ref[pl.ds(base + i, width, stride=stride)].T


def on_device(sections, count, views_data, start, psf_table, psf_index):
    f32, bf16 = jnp.float32, jnp.bfloat16
    planes, width_x, width_y = start.shape
    taps = psf_table.shape[2]
    reach = taps - 1
    pad = reach // 2
    blocks = count // 2
    rows = width_y // 4
    depth = 2 * planes
    wide, deep = rows + 2 * reach, depth + 2 * reach
    tall, outer = rows + 2 * pad, depth + 2 * pad
    shape = jax.ShapeDtypeStruct
    dma = lambda n: [pltpu.SemaphoreType.DMA((n,)), pltpu.SemaphoreType.DMA((n,))]
    stride = odd_stride(planes)

    kern = jnp.sum(jnp.where(jnp.arange(psf_table.shape[0])[:, None, None] == psf_index[0], psf_table, 0.0), axis=0)
    kern = kern / jnp.sum(kern, axis=-1, keepdims=True)
    kern = jnp.pad(kern, ((0, 8 - kern.shape[0]), (0, 128 - taps)))

    est, data, *matrices = pl.pallas_call(
        functools.partial(setup_kernel, blocks, taps, rows),
        out_shape=[
            shape((wide, deep, width_x), f32),
            shape((2, outer, tall, width_x), f32),
            shape((2, 2 * outer, 2 * deep), bf16),
            shape((2, 2 * width_x, 2 * width_x), bf16),
            shape((2, 2 * tall, 2 * wide), bf16),
            shape((2, 2 * rows, 2 * tall), bf16),
            shape((2, 2 * width_x, 2 * width_x), bf16),
            shape((2, 2 * depth, 2 * outer), bf16),
        ],
        in_specs=[ANY, ANY, VMEM],
        out_specs=[VMEM] * 8,
        scratch_shapes=[
            pltpu.VMEM(start.shape, f32),
            pltpu.VMEM(start.shape, f32),
            pltpu.VMEM(((width_y + 2 * reach) * stride, width_x), f32),
            pltpu.VMEM((planes, width_y + 2 * pad, width_x), f32),
            pltpu.VMEM((2, 8, 128), f32),
            pltpu.SemaphoreType.DMA((2,)),
            *dma(1), *dma(6), *dma(6), *dma(4),
        ],
        compiler_params=pltpu.CompilerParams(
            collective_id=0, has_side_effects=True, vmem_limit_bytes=40 * MIB
        ),
    )(views_data[0], start, kern)

    for step in range(ITERS):
        product = pl.pallas_call(
            iteration_kernel,
            out_shape=shape((rows, depth, width_x), f32),
            in_specs=[VMEM] * 8,
            out_specs=VMEM,
            scratch_shapes=[
                pltpu.VMEM((2, wide * odd_stride(outer), width_x), f32),
                pltpu.VMEM((2, outer * odd_stride(rows), width_x), f32),
            ],
            compiler_params=pltpu.CompilerParams(vmem_limit_bytes=40 * MIB),
        )(est, data, *matrices)
        if step < ITERS - 1:
            est = pl.pallas_call(
                functools.partial(middle_kernel, blocks),
                out_shape=shape(est.shape, f32),
                in_specs=[VMEM] * 2,
                out_specs=VMEM,
                scratch_shapes=[
                    pltpu.VMEM(product.shape, f32), *dma(4), *dma(2), *dma(4), *dma(4),
                ],
                compiler_params=pltpu.CompilerParams(
                    collective_id=1, has_side_effects=True, vmem_limit_bytes=40 * MIB
                ),
            )(product, est)

    gathered = pl.pallas_call(
        functools.partial(last_kernel, blocks),
        out_shape=shape((width_y, stride, width_x), f32),
        in_specs=[VMEM] * 2,
        out_specs=VMEM,
        scratch_shapes=[
            pltpu.VMEM(product.shape, f32), pltpu.VMEM(product.shape, f32), *dma(4), *dma(3), *dma(3),
        ],
        compiler_params=pltpu.CompilerParams(
            collective_id=2, has_side_effects=True, vmem_limit_bytes=40 * MIB
        ),
    )(product, est)
    return pl.pallas_call(
        output_kernel,
        grid=(planes // 4,),
        out_shape=shape(start.shape, f32),
        in_specs=[VMEM],
        out_specs=pl.BlockSpec((4, width_x, width_y), lambda i: (i, 0, 0)),
        compiler_params=pltpu.CompilerParams(vmem_limit_bytes=40 * MIB),
    )(gathered.reshape(width_y * stride, width_x))


def solution(mesh):
    return jax.shard_map(
        functools.partial(on_device, mesh.shape["view"], mesh.shape["gz"]),
        mesh=mesh,
        in_specs=(P("view", "gz", None, None), P("gz", None, None), P(), P("view")),
        out_specs=P("gz", None, None),
        check_vma=False,
    )
```

time: 278 us -> 176 us (0.63)
  Pallas kernels: 62.9 us -> 162 us
  waiting for transfers between devices: 91.1 us -> 0 us
  starting transfers between devices: 85.1 us -> 0 us
  other arithmetic: 16.7 us -> 0.96 us
  local copies, waits for them, and re-layouts: 17.2 us -> 10.5 us
    pallas_call x12 -> x6, Pallas kernels: 62.9 us -> 162 us  [the longest x1 58.6 us: on_device(): pl.pallas_call(functools.partial(setup_kernel, blocks, taps, rows), out_s...]
    ppermute x36 -> x0, waiting for transfers between devices: 91.1 us -> none  [move(): return lax.ppermute(value, AXES, pairs)]
    ppermute x36 -> x0, starting transfers between devices: 85.1 us -> none  [move(): return lax.ppermute(value, AXES, pairs)]
    unnamed x48 -> x12, local copies, waits for them, and re-layouts: 4.67 us -> 10.5 us
    mul x3 -> x0, other arithmetic: 4.53 us -> none  [the longest x2 3.53 us: on_device(): estimate = estimate * jnp.sqrt(jnp.sqrt(total))]
    mul x4 -> x0, local copies, waits for them, and re-layouts: 4.51 us -> none  [x_matrix(): eye[:, None, :, None] * one[None, :, None, :]]
    dynamic_slice x3 -> x0, local copies, waits for them, and re-layouts: 4.19 us -> none  [the longest x1 3.06 us: rows_for(): return lax.dynamic_slice_in_dim(block, strip_of(a, b) * share, share, 1)]
    concatenate x6 -> x0, other arithmetic: 4 us -> none  [the longest x3 2.15 us: in_order(): jnp.concatenate([jnp.where(first_is_mine, mine, theirs), jnp.where(first_...]
  transfers between devices with their start and end apart: 36 -> 0, of which waited for: 16 -> 0; matrix products, arithmetic and copies ran while one was open for 7% -> 0% of each run, Pallas kernels for 13% -> 0%
where the time goes in v1:
time: 176 us; the launch traced here: 174 us
  Pallas kernels  162 us (92%)
  local copies, waits for them, and re-layouts  10.5 us (6%)
    pallas_call x1, Pallas kernels, on_device(): pl.pallas_call(functools.partial(setup_kernel, blocks, taps, rows), out_s...  58.6 us
    pallas_call x2, Pallas kernels, on_device(): pl.pallas_call(iteration_kernel, out_shape=shape((rows, depth, width_x),...  50.7 us
    pallas_call x1, Pallas kernels, on_device(): pl.pallas_call(functools.partial(last_kernel, blocks), out_shape=shape((w...  26.6 us
    pallas_call x1, Pallas kernels, on_device(): pl.pallas_call(functools.partial(middle_kernel, blocks), out_shape=shape(...  23.3 us
    unnamed x12, local copies, waits for them, and re-layouts  10.5 us

profile of v1, /device:TPU:17, one launch (start us, length us, event | category | flops | bytes accessed | tf_op | source)
XLA Modules:
  0.0 174.1 jit_solution(8714509474999419019)
XLA Ops:
  0.7 0.9 select_reduce_fusion
  1.5 0.1 broadcast_divide_fusion
  1.6 0.0 copy-start.4
  1.6 1.9 %copy-done.4 = f32[1,16,128,384]{3,2,1,0:T(8,128)S(1)} copy-done((f32[1,16,128,384]{3,2,1,0:T(8,128)S(1)}, f32[1,16,128,384]{3,2,1,0:T(8,128)}, u32[]{:S(2)}) %copy-start.4) | copy-done | bytes 3145752
  3.5 0.0 copy-start.5
  3.5 1.9 %copy-done.5 = f32[16,128,384]{2,1,0:T(8,128)S(1)} copy-done((f32[16,128,384]{2,1,0:T(8,128)S(1)}, f32[16,128,384]{2,1,0:T(8,128)}, u32[]{:S(2)}) %copy-start.5) | copy-done | bytes 3145752
  5.4 58.6 %shard_map.46 = (f32[128,64,128]{2,1,0:T(8,128)S(1)}, f32[2,48,112,128]{3,2,1,0:T(8,128)}, bf16[2,96,128]{2,1,0:T(8,128)(2,1)S(1)}, bf16[2,256,256]{2,1,0:T(8,12...) custom-call(f32[16,128,384]{2,1,0:T(8,128)S(1)} %bitcast.5, ...), custom_call_target="tpu_custom_call" | custom-call | tf_op jit(solution)/shard_map/pallas_call | solution.py:540
  64.0 0.0 copy-start
  64.0 2.6 %copy-done = f32[2,48,112,128]{3,2,1,0:T(8,128)S(1)} copy-done((f32[2,48,112,128]{3,2,1,0:T(8,128)S(1)}, f32[2,48,112,128]{3,2,1,0:T(8,128)}, u32[]{:S(2)}) %copy-start) | copy-done | bytes 5505048
  66.5 25.4 %shard_map.47.product_ref = f32[96,32,128]{2,1,0:T(8,128)S(1)} custom-call(f32[128,64,128]{2,1,0:T(8,128)S(1)} %get-tuple-element.13.est_ref.old_ref, f32[2,48,112,128]{3,2,1,0:T(8,128)S(1)} %copy-done, bf16[2,96,128]{2,1,0:T(8,128)(2,1)S(1)} %get-tuple-element.15.lz_ref, bf16[2,256,256]{2,1,0:T(8,128)(2,1)S(1)} %get-tuple-element.16.x_ref, ...), custom_call_target="tpu_custom_call" | custom-call | tf_op jit(solution)/shard_map/pallas_call | solution.py:569
  91.9 0.0 copy-start.2
  91.9 2.0 %copy-done.2 = f32[128,64,128]{2,1,0:T(8,128)} copy-done((f32[128,64,128]{2,1,0:T(8,128)}, f32[128,64,128]{2,1,0:T(8,128)S(1)}, u32[]{:S(2)}) %copy-start.2) | copy-done | bytes 4194328
  93.9 0.0 copy-start.3
  93.9 2.2 %copy-done.3 = f32[128,64,128]{2,1,0:T(8,128)S(1)} copy-done((f32[128,64,128]{2,1,0:T(8,128)S(1)}, f32[128,64,128]{2,1,0:T(8,128)}, u32[]{:S(2)}) %copy-start.3) | copy-done | bytes 4194328
  96.1 0.0 copy-start.1
  96.1 23.3 %shard_map.48.est_ref.old_ref = f32[128,64,128]{2,1,0:T(8,128)S(1)} custom-call(f32[96,32,128]{2,1,0:T(8,128)S(1)} %shard_map.47.product_ref, f32[128,64,128]{2,1,0:T(8,128)S(1)} %copy-done.3), custom_call_target="tpu_custom_call" | custom-call | tf_op jit(solution)/shard_map/pallas_call | solution.py:581
  119.5 0.0 copy-done.1
  119.5 25.4 %shard_map.49.product_ref = f32[96,32,128]{2,1,0:T(8,128)S(1)} custom-call(f32[128,64,128]{2,1,0:T(8,128)S(1)} %shard_map.48.est_ref.old_ref, f32[2,48,112,128]{3,2,1,0:T(8,128)S(1)} %copy-done.1, bf16[2,96,128]{2,1,0:T(8,128)(2,1)S(1)} %get-tuple-element.15.lz_ref, bf16[2,256,256]{2,1,0:T(8,128)(2,1)S(1)} %get-tuple-element.16.x_ref, ...), custom_call_target="tpu_custom_call" | custom-call | tf_op jit(solution)/shard_map/pallas_call | solution.py:569
  144.8 26.6 %shard_map.50 = f32[384,24,128]{2,1,0:T(8,128)S(1)} custom-call(f32[96,32,128]{2,1,0:T(8,128)S(1)} %shard_map.49.product_ref, f32[128,64,128]{2,1,0:T(8,128)S(1)} %shard_map.48.est_ref.old_ref), custom_call_target="tpu_custom_call" | custom-call | tf_op jit(solution)/shard_map/pallas_call | solution.py:594
  171.5 2.6 %shard_map.51 = f32[16,128,384]{2,1,0:T(8,128)} custom-call(f32[9216,128]{1,0:T(8,128)S(1)} %bitcast.4), custom_call_target="tpu_custom_call" | custom-call | tf_op jit(solution)/shard_map/pallas_call | solution.py:606
  (2 shorter events, 0.0 us)
Async XLA Ops:
  1.6 1.9 %copy-start.4 = (f32[1,16,128,384]{3,2,1,0:T(8,128)S(1)}, f32[1,16,128,384]{3,2,1,0:T(8,128)}, u32[]{:S(2)}) copy-start(f32[1,16,128,384]{3,2,1,0:T(8,128)} %param.4) | copy-start | bytes 9437188
  3.5 1.9 %copy-start.5 = (f32[16,128,384]{2,1,0:T(8,128)S(1)}, f32[16,128,384]{2,1,0:T(8,128)}, u32[]{:S(2)}) copy-start(f32[16,128,384]{2,1,0:T(8,128)} %start_hbm.1) | copy-start | bytes 9437188
  64.0 2.6 %copy-start = (f32[2,48,112,128]{3,2,1,0:T(8,128)S(1)}, f32[2,48,112,128]{3,2,1,0:T(8,128)}, u32[]{:S(2)}) copy-start(f32[2,48,112,128]{3,2,1,0:T(8,128)} %get-tuple-element.14.data_ref) | copy-start | bytes 16515076
  91.9 2.0 %copy-start.2 = (f32[128,64,128]{2,1,0:T(8,128)}, f32[128,64,128]{2,1,0:T(8,128)S(1)}, u32[]{:S(2)}) copy-start(f32[128,64,128]{2,1,0:T(8,128)S(1)} %get-tuple-element.13.est_ref.old_ref) | copy-start | bytes 12582916
  93.9 2.2 %copy-start.3 = (f32[128,64,128]{2,1,0:T(8,128)S(1)}, f32[128,64,128]{2,1,0:T(8,128)}, u32[]{:S(2)}) copy-start(f32[128,64,128]{2,1,0:T(8,128)} %copy-done.2) | copy-start | bytes 12582916
  96.1 23.3 %copy-start.1 = (f32[2,48,112,128]{3,2,1,0:T(8,128)S(1)}, f32[2,48,112,128]{3,2,1,0:T(8,128)}, u32[]{:S(2)}) copy-start(f32[2,48,112,128]{3,2,1,0:T(8,128)} %get-tuple-element.14.data_ref) | copy-start | bytes 16515076

commit v2 on v1

v2 whole, which is shorter than its diff:
```python
import functools
import jax
import jax.numpy as jnp
from jax import lax
from jax.experimental import pallas as pl
from jax.experimental.pallas import tpu as pltpu
from jax.sharding import PartitionSpec as P

ITERS = 2
GROUP = 32
MESH = pl.DeviceIdType.MESH
VMEM = pl.BlockSpec(memory_space=pltpu.VMEM)
HBM = pl.BlockSpec(memory_space=pltpu.HBM)
VMEM_LIMIT = 56
MIB = 1024 * 1024


def split(value):
    high = value.astype(jnp.bfloat16)
    return high, (value - high.astype(jnp.float32)).astype(jnp.bfloat16)


def dot(lhs, rhs):
    return jnp.dot(lhs, rhs, preferred_element_type=jnp.float32)


def odd_stride(rows):
    return rows + 8 if (rows // 8) % 2 == 0 else rows


class Place:
    def __init__(self, blocks):
        view, gz = lax.axis_index("view"), lax.axis_index("gz")
        self.blocks = blocks
        self.a, self.c = view // 2, view % 2
        self.k, self.b = gz // 2, gz % 2
        self.strip = self.strip_of(self.a, self.b)

    @staticmethod
    def strip_of(a, b):
        return 2 * a + (a + b) % 2

    def device(self, a=None, c=None, k=None, b=None):
        a = self.a if a is None else a
        c = self.c if c is None else c
        k = self.k if k is None else k
        b = self.b if b is None else b
        return (2 * a + c, 2 * k + b)

    def of_strip(self, strip):
        return self.device(a=strip // 2, b=(strip % 2 + strip // 2) % 2)

    def partner(self):
        return self.device(c=1 - self.c)

    def others(self):
        a, b = self.a, self.b
        return ((a, 1 - b), (1 - a, b), (1 - a, 1 - b))


def remote(src, dst, sems, index, device):
    send, recv = sems
    return pltpu.make_async_remote_copy(
        src_ref=src, dst_ref=dst, send_sem=send.at[index], recv_sem=recv.at[index],
        device_id=device, device_id_type=MESH,
    )


def greet(here):
    barrier = pltpu.get_barrier_semaphore()

    def signal(device):
        pl.semaphore_signal(barrier, inc=1, device_id=device, device_id_type=MESH)

    signal(here.partner())
    count = 1
    for a, b in here.others():
        signal(here.device(a=a, b=b))
        count += 1
    for step in (-1, 1):
        there = here.k + step
        inside = (there >= 0) & (there < here.blocks)
        pl.when(inside)(functools.partial(lambda there: signal(here.device(k=there)), there))
        count = count + inside.astype(jnp.int32)
    pl.semaphore_wait(barrier, count)


def band(taps, outputs, inputs, sign, shift):
    at = sign * (
        lax.broadcasted_iota(jnp.int32, (outputs, inputs), 1)
        - lax.broadcasted_iota(jnp.int32, (outputs, inputs), 0)
    ) + shift
    total = jnp.zeros((outputs, inputs), jnp.float32)
    for tap, value in enumerate(taps):
        total = jnp.where(at == tap, value, total)
    return total


def write_left(ref, index, matrix):
    high, low = split(matrix)
    rows, depth = matrix.shape
    top = jnp.concatenate([high, high], axis=1)
    bottom = jnp.concatenate([low, low], axis=1)
    ref[index] = jnp.concatenate([top, bottom], axis=0)


def write_right(ref, index, matrix):
    high, low = split(matrix)
    half = jnp.concatenate([high, low], axis=1)
    ref[index] = jnp.concatenate([half, half], axis=0)


def write_matrices(kern_ref, taps, refs):
    lz_ref, x_ref, ly_ref, lyb_ref, xb_ref, lzb_ref = refs
    reach = taps - 1
    pad = reach // 2
    for which in range(2):
        rows = kern_ref[which]
        kz, kx, ky = ([rows[r:r + 1, t:t + 1] for t in range(taps)] for r in range(3))
        outputs, inputs = lz_ref.shape[1] // 2, lz_ref.shape[2] // 2
        write_left(lz_ref, which, band(kz, outputs, inputs, 1, 0))
        write_right(x_ref, which, band(kx, x_ref.shape[1] // 2, x_ref.shape[2] // 2, -1, pad))
        write_left(ly_ref, which, band(ky, ly_ref.shape[1] // 2, ly_ref.shape[2] // 2, 1, 0))
        write_left(lyb_ref, which, band(ky, lyb_ref.shape[1] // 2, lyb_ref.shape[2] // 2, -1, reach))
        write_right(xb_ref, which, band(kx, xb_ref.shape[1] // 2, xb_ref.shape[2] // 2, 1, pad))
        write_left(lzb_ref, which, band(kz, lzb_ref.shape[1] // 2, lzb_ref.shape[2] // 2, -1, reach))


def sides(product):
    half = product.shape[1] // 2
    return product[:, :half] + product[:, half:]


def stack(product):
    half = product.shape[0] // 2
    return product[:half] + product[half:]


def cut(value, count):
    lanes = value.shape[1] // count
    return [value[:, i * lanes:(i + 1) * lanes] for i in range(count)]


def stacked(values):
    return jnp.concatenate([jnp.concatenate(split(value), axis=0) for value in values], axis=1)


def beside(pieces):
    return jnp.concatenate(split(jnp.concatenate(pieces, axis=0)), axis=1)


def root(value):
    return jnp.sqrt(jnp.sqrt(value))


def forward_rows(base, count, est_ref, lz_ref, x_ref, t_ref):
    outer = lz_ref.shape[1] // 2
    stride = t_ref.shape[1] // est_ref.shape[0]
    left = lz_ref[...].reshape(4 * outer, lz_ref.shape[2])
    both = dot(left, stacked([est_ref[base + i] for i in range(count)]))
    for which in range(2):
        along_z = stack(both[2 * outer * which:2 * outer * (which + 1)])
        along_x = sides(dot(beside(cut(along_z, count)), x_ref[which]))
        for i in range(count):
            t_ref[which, pl.ds(pl.multiple_of((base + i) * stride, 8), outer)] = along_x[i * outer:(i + 1) * outer]


def ratio_planes(planes, data_ref, ly_ref, lyb_ref, xb_ref, t_ref, s_ref):
    count = len(planes)
    wide, rows = ly_ref.shape[2] // 2, lyb_ref.shape[1] // 2
    t_stride = t_ref.shape[1] // wide
    s_stride = s_ref.shape[1] // data_ref.shape[1]
    for which in range(2):
        right = stacked([t_ref[which, pl.ds(plane, wide, stride=t_stride)] for plane in planes])
        blurred = stack(dot(ly_ref[which], right))
        data = jnp.concatenate([data_ref[which, plane] for plane in planes], axis=1)
        right = jnp.concatenate(split(data / blurred), axis=0)
        along_y = stack(dot(lyb_ref[which], right))
        along_x = sides(dot(beside(cut(along_y, count)), xb_ref[which]))
        for i, plane in enumerate(planes):
            s_ref[which, pl.ds(pl.multiple_of(plane * s_stride, 8), rows)] = along_x[i * rows:(i + 1) * rows]


def back_rows(base, count, lzb_ref, s_ref, product_ref):
    outer = lzb_ref.shape[2] // 2
    stride = s_ref.shape[1] // outer
    both = []
    for which in range(2):
        right = stacked([s_ref[which, pl.ds(base + i, outer, stride=stride)] for i in range(count)])
        both.append(stack(dot(lzb_ref[which], right)))
    for i, piece in enumerate(cut(both[0] * both[1], count)):
        product_ref[base + i] = piece


def whole_kernel(blocks, strip_rows, data_hbm, start_hbm, table_ref, index_ref,
                 all_ref,
                 sbuf, dbuf, ts_ref, td_ref, kern_ref, est_ref, est2_ref, data_ref,
                 lz_ref, x_ref, ly_ref, lyb_ref, xb_ref, lzb_ref, t_ref, s_ref,
                 product_ref, other_ref, other2_ref,
                 load_sem, kern_s, kern_r, e_s, e_r, d_s, d_r, h_s, h_r,
                 p_s, p_r, y_s, y_r, z_s, z_r, q_s, q_r, f_s, f_r, g_s, g_r, o_s, o_r, w_s, w_r):
    here = Place(blocks)
    planes, width_x, width_y = start_hbm.shape
    taps = table_ref.shape[2]
    reach = taps - 1
    pad = reach // 2
    depth = 2 * planes
    rows = strip_rows
    wide = rows + 2 * reach
    tall = rows + 2 * pad
    stride = ts_ref.shape[0] // (width_y + 2 * reach)
    half = wide // 2
    k, a, b, c, strip = here.k, here.a, here.b, here.c, here.strip
    below, above = k > 0, k < blocks - 1
    unless = lambda condition: pl.when(jnp.logical_not(condition))
    load_start = pltpu.make_async_copy(start_hbm, sbuf, load_sem.at[0])
    load_data = pltpu.make_async_copy(data_hbm, dbuf, load_sem.at[1])
    load_start.start()
    load_data.start()
    ts3 = ts_ref.reshape(width_y + 2 * reach, stride, width_x)

    table = table_ref[...]
    kern = jnp.zeros(table.shape[1:], jnp.float32)
    for i in range(table.shape[0]):
        kern = jnp.where(index_ref[0] == i, table[i], kern)
    kern = kern / jnp.sum(kern, axis=-1, keepdims=True)
    kern_ref[a] = jnp.zeros(kern_ref.shape[1:], jnp.float32)
    kern_ref[a, pl.ds(0, 3), pl.ds(0, taps)] = kern
    ts_ref[pl.ds(0, reach * stride)] = jnp.zeros((reach * stride, width_x), jnp.float32)
    ts_ref[pl.ds((width_y + reach) * stride, reach * stride)] = jnp.zeros((reach * stride, width_x), jnp.float32)
    for z in range(planes):
        td_ref[z, pl.ds(0, pad)] = jnp.zeros((pad, width_x), jnp.float32)
        td_ref[z, pl.ds(pad + width_y, pad)] = jnp.zeros((pad, width_x), jnp.float32)
    greet(here)

    load_start.wait()

    @pl.loop(0, planes)
    def _(z):
        ts_ref[pl.ds(reach * stride + z, width_y, stride=stride)] = sbuf[z].T

    mine = pl.multiple_of(reach + planes * b, 8)
    theirs = pl.multiple_of(reach + planes * (1 - b), 8)
    rows_c = pl.ds(half * c, half)
    e_copy = remote(
        ts3.at[pl.ds(rows * here.strip_of(a, 1 - b) + half * c, half), pl.ds(0, planes)],
        est_ref.at[rows_c, pl.ds(mine, planes)], (e_s, e_r), 0, here.device(b=1 - b),
    )
    e_copy.start()
    kern_copy = remote(kern_ref.at[a], kern_ref.at[a], (kern_s, kern_r), 0, here.device(a=1 - a))
    kern_copy.start()

    load_data.wait()

    @pl.loop(0, planes)
    def _(z):
        td_ref[z, pl.ds(pad, width_y)] = dbuf[z].T

    d_copies = []
    for part, (first, size) in enumerate(((b * (planes - pad), pad), ((1 - b) * pad, planes - pad))):
        for kind, (oa, ob) in enumerate(here.others()):
            copy = remote(
                td_ref.at[pl.ds(first, size), pl.ds(rows * here.strip_of(oa, ob), tall)],
                data_ref.at[a, pl.ds(pad + planes * b + first, size)],
                (d_s, d_r), 3 * part + kind, here.device(a=oa, b=ob),
            )
            copy.start()
            d_copies.append(copy)

    @pl.loop(0, wide)
    def _(row):
        est_ref[row, pl.ds(mine, planes)] = ts3[rows * strip + row, pl.ds(0, planes)]

    @pl.loop(0, planes)
    def _(z):
        data_ref[a, pad + planes * b + z] = td_ref[z, pl.ds(pl.multiple_of(rows * strip, 8), tall)]

    def zero(ref, first_row, count, first, size):
        @pl.loop(0, count)
        def _(row):
            ref[first_row + row, pl.ds(first, size)] = jnp.zeros((size, width_x), jnp.float32)

    unless(below)(lambda: zero(est_ref, 0, wide, 0, reach))
    unless(above)(lambda: zero(est_ref, 0, wide, reach + depth, reach))

    def halo(kind, oa, ob):
        to = k + 2 * ob - 1
        source = k + 1 - 2 * ob
        place = (1 - ob) * (depth + pad)
        copy = remote(
            data_ref.at[oa, pl.ds(pad + ob * (depth - pad), pad)], data_ref.at[oa, pl.ds(place, pad)],
            (h_s, h_r), kind, here.device(k=to),
        )
        sends = (to >= 0) & (to < blocks)
        gets = (source >= 0) & (source < blocks)
        unless(gets)(lambda: zero(data_ref.at[oa], place, pad, 0, tall))
        pl.when(sends)(copy.start)
        return copy, sends, gets

    halos = [halo(3, a, b)]

    kern_copy.wait()
    write_matrices(kern_ref, taps, (lz_ref, x_ref, ly_ref, lyb_ref, xb_ref, lzb_ref))

    e_copy.wait()
    relay = remote(
        est_ref.at[rows_c, pl.ds(theirs, planes)], est_ref.at[rows_c, pl.ds(theirs, planes)],
        (e_s, e_r), 1, here.partner(),
    )
    bottom, top = pl.ds(0, reach), pl.ds(reach + depth, reach)
    first, last = pl.ds(reach, reach), pl.ds(depth, reach)
    up = remote(est_ref.at[rows_c, last], est_ref.at[rows_c, bottom], (e_s, e_r), 2, here.device(k=k + 1))
    down = remote(est_ref.at[rows_c, first], est_ref.at[rows_c, top], (e_s, e_r), 3, here.device(k=k - 1))
    from_below = remote(est_ref.at[rows_c, bottom], est_ref.at[rows_c, bottom], (e_s, e_r), 4, here.partner())
    from_above = remote(est_ref.at[rows_c, top], est_ref.at[rows_c, top], (e_s, e_r), 5, here.partner())
    pl.when(above)(up.start)
    pl.when(below)(down.start)
    relay.start()

    @pl.when(below)
    def _():
        up.wait_recv()
        from_below.start()

    @pl.when(above)
    def _():
        down.wait_recv()
        from_above.start()

    pl.when(above)(up.wait_send)
    pl.when(below)(down.wait_send)
    relay.wait()
    pl.when(below)(from_below.wait)
    pl.when(above)(from_above.wait)

    @pl.loop(0, wide // GROUP)
    def _(step):
        forward_rows(step * GROUP, GROUP, est_ref, lz_ref, x_ref, t_ref)

    def back_planes(base, other):
        ratio_planes(
            [base + i for i in range(pad)] + [other + i for i in range(pad)],
            data_ref, ly_ref, lyb_ref, xb_ref, t_ref, s_ref,
        )

    steps = planes // pad + 1
    for kind, (oa, ob) in enumerate(here.others()):
        d_copies[kind].wait_recv()
        halos.append(halo(kind, oa, ob))

    @pl.loop(0, steps)
    def _(step):
        @pl.when(step == 1)
        def _():
            for copy in d_copies[3:]:
                copy.wait_recv()

        @pl.when(step == steps - 1)
        def _():
            for copy, sends, gets in halos:
                pl.when(gets)(copy.wait_recv)

        outside, edge = step == steps - 1, step == 0
        back_planes(
            jnp.where(outside, 0, jnp.where(edge, pad, 2 * pad * step)),
            jnp.where(outside, depth + pad, jnp.where(edge, depth, 2 * pad * step + pad)),
        )

    chunks = rows // reach
    inside = pl.ds(reach, depth)
    left, right = strip > 0, strip < 3

    def chunk_of(i):
        middle = jnp.where(i == 0, 1, jnp.where(i == 1, chunks, i))
        return jnp.where(i == chunks, 0, jnp.where(i == chunks + 1, chunks + 1, middle))

    def swap(q):
        at = pl.ds(reach * q, reach)
        return remote(product_ref.at[at], other_ref.at[at], (p_s, p_r), q, here.partner())

    @pl.loop(0, chunks)
    def _(i):
        q = chunk_of(i) - 1
        back_rows(reach * q, reach, lzb_ref, s_ref, product_ref)
        swap(q).start()

    unless(left)(lambda: zero(est2_ref, 0, reach, reach, depth))
    unless(right)(lambda: zero(est2_ref, reach + rows, reach, reach, depth))
    unless(below)(lambda: zero(est2_ref, 0, wide, 0, reach))
    unless(above)(lambda: zero(est2_ref, 0, wide, reach + depth, reach))

    to_left = remote(
        est2_ref.at[pl.ds(reach, reach), inside], est2_ref.at[pl.ds(reach + rows, reach), inside],
        (y_s, y_r), 0, here.of_strip(strip - 1),
    )
    to_right = remote(
        est2_ref.at[pl.ds(rows, reach), inside], est2_ref.at[pl.ds(0, reach), inside],
        (y_s, y_r), 1, here.of_strip(strip + 1),
    )
    to_block = k + 1 - 2 * c
    z_sends = (to_block >= 0) & (to_block < blocks)
    z_gets = (k - 1 + 2 * c >= 0) & (k - 1 + 2 * c < blocks)
    q_gets = (k + 1 - 2 * c >= 0) & (k + 1 - 2 * c < blocks)
    z_from = pl.multiple_of(reach + (1 - c) * (depth - reach), 8)
    z_to = pl.multiple_of(c * (reach + depth), 8)

    def along_z(e):
        at = pl.ds(reach * e, reach)
        return remote(
            est2_ref.at[at, pl.ds(z_from, reach)], est2_ref.at[at, pl.ds(z_to, reach)],
            (z_s, z_r), e, here.device(k=to_block),
        )

    def across(e):
        at = pl.ds(reach * e, reach)
        return remote(
            est2_ref.at[at, pl.ds(z_to, reach)], est2_ref.at[at, pl.ds(z_to, reach)],
            (q_s, q_r), e, here.partner(),
        )

    @pl.loop(0, chunks)
    def _(i):
        e = chunk_of(i)
        q = e - 1
        swap(q).wait_recv()

        @pl.loop(0, reach)
        def _(r):
            row = reach * q + r
            factor = root(product_ref[row] * other_ref[row])
            est2_ref[reach + row, inside] = est_ref[reach + row, inside] * factor

        pl.when((i == 0) & left)(to_left.start)
        pl.when((i == 1) & right)(to_right.start)
        pl.when(z_sends)(along_z(e).start)

    pl.when(left)(to_right.wait_recv)
    pl.when(right)(to_left.wait_recv)
    pl.when(z_sends)(along_z(0).start)
    pl.when(z_sends)(along_z(chunks + 1).start)

    @pl.loop(0, chunks + 3)
    def _(i):
        @pl.when((i < chunks + 2) & z_gets)
        def _():
            e = chunk_of(i)
            along_z(e).wait_recv()
            across(e).start()

        @pl.when(i >= 1)
        def _():
            e = chunk_of(i - 1)
            pl.when(q_gets)(across(e).wait_recv)
            forward_rows(reach * e, reach, est2_ref, lz_ref, x_ref, t_ref)

    @pl.loop(0, chunks)
    def _(q):
        swap(q).wait_send()

    @pl.loop(0, steps)
    def _(step):
        back_planes(2 * pad * step, 2 * pad * step + pad)

    part = reach // 2

    def last_swap(q):
        at = pl.ds(reach * q + part * (1 - c), part)
        return remote(product_ref.at[at], other2_ref.at[at], (f_s, f_r), q, here.partner())

    def gather(q, kind, oa, ob):
        return remote(
            other2_ref.at[pl.ds(reach * q + part * c, part), pl.ds(pl.multiple_of(planes * ob, 8), planes)],
            all_ref.at[pl.ds(rows * strip + reach * q + part * c, part)],
            (g_s, g_r), 3 * q + kind, here.device(a=oa, b=ob),
        )

    def own(q):
        return remote(
            other2_ref.at[pl.ds(reach * q + part * c, part), pl.ds(pl.multiple_of(planes * b, 8), planes)],
            all_ref.at[pl.ds(rows * strip + reach * q + part * c, part)],
            (o_s, o_r), q, here.partner(),
        )

    def onward(q, kind, oa, ob):
        at = pl.ds(rows * here.strip_of(oa, ob) + reach * q + part * c, part)
        return remote(all_ref.at[at], all_ref.at[at], (w_s, w_r), 3 * q + kind, here.partner())

    @pl.loop(0, chunks)
    def _(q):
        back_rows(reach * q, reach, lzb_ref, s_ref, product_ref)
        last_swap(q).start()

    @pl.loop(0, chunks)
    def _(q):
        last_swap(q).wait_recv()

        @pl.loop(0, part)
        def _(r):
            row = reach * q + part * c + r
            factor = root(product_ref[row] * other2_ref[row])
            other2_ref[row] = est2_ref[reach + row, inside] * factor
            all_ref[rows * strip + row] = other2_ref[row, pl.ds(pl.multiple_of(planes * b, 8), planes)]

        for kind in (2, 0, 1):
            gather(q, kind, *here.others()[kind]).start()
        own(q).start()

    @pl.loop(0, chunks)
    def _(q):
        for kind in range(3):
            gather(q, kind, *here.others()[kind]).wait_recv()
            onward(q, kind, *here.others()[kind]).start()

    @pl.loop(0, chunks)
    def _(q):
        last_swap(q).wait_send()
        own(q).wait()
        for kind in range(3):
            gather(q, kind, *here.others()[kind]).wait_send()
            onward(q, kind, *here.others()[kind]).wait()

    for copy in d_copies:
        copy.wait_send()
    for copy, sends, gets in halos:
        pl.when(sends)(copy.wait_send)
    pl.when(left)(to_left.wait_send)
    pl.when(right)(to_right.wait_send)

    @pl.loop(0, chunks + 2)
    def _(e):
        pl.when(z_sends)(along_z(e).wait_send)
        pl.when(z_gets)(across(e).wait_send)


def output_kernel(all_ref, out_ref):
    group, lanes, width = out_ref.shape
    stride = all_ref.shape[0] // width
    base = pl.program_id(0) * group
    for i in range(group):
        out_ref[i] = all_ref[pl.ds(base + i, width, stride=stride)].T


def on_device(blocks, views_data, start, psf_table, psf_index):
    f32, bf16 = jnp.float32, jnp.bfloat16
    planes, width_x, width_y = start.shape
    reach = psf_table.shape[2] - 1
    pad = reach // 2
    rows = width_y // 4
    depth = 2 * planes
    wide, deep = rows + 2 * reach, depth + 2 * reach
    tall, outer = rows + 2 * pad, depth + 2 * pad
    chunks = rows // reach
    dma = lambda n: [pltpu.SemaphoreType.DMA((n,)), pltpu.SemaphoreType.DMA((n,))]

    gathered = pl.pallas_call(
        functools.partial(whole_kernel, blocks, rows),
        out_shape=jax.ShapeDtypeStruct((width_y, planes, width_x), f32),
        in_specs=[HBM, HBM, VMEM, pl.BlockSpec(memory_space=pltpu.SMEM)],
        out_specs=VMEM,
        scratch_shapes=[
            pltpu.VMEM(start.shape, f32),
            pltpu.VMEM(start.shape, f32),
            pltpu.VMEM(((width_y + 2 * reach) * odd_stride(planes), width_x), f32),
            pltpu.VMEM((planes, width_y + 2 * pad, width_x), f32),
            pltpu.VMEM((2, 8, 128), f32),
            pltpu.VMEM((wide, deep, width_x), f32),
            pltpu.VMEM((wide, deep, width_x), f32),
            pltpu.VMEM((2, outer, tall, width_x), f32),
            pltpu.VMEM((2, 2 * outer, 2 * deep), bf16),
            pltpu.VMEM((2, 2 * width_x, 2 * width_x), bf16),
            pltpu.VMEM((2, 2 * tall, 2 * wide), bf16),
            pltpu.VMEM((2, 2 * rows, 2 * tall), bf16),
            pltpu.VMEM((2, 2 * width_x, 2 * width_x), bf16),
            pltpu.VMEM((2, 2 * depth, 2 * outer), bf16),
            pltpu.VMEM((2, wide * odd_stride(outer), width_x), f32),
            pltpu.VMEM((2, outer * odd_stride(rows), width_x), f32),
            pltpu.VMEM((rows, depth, width_x), f32),
            pltpu.VMEM((rows, depth, width_x), f32),
            pltpu.VMEM((rows, depth, width_x), f32),
            pltpu.SemaphoreType.DMA((2,)),
            *dma(1), *dma(6), *dma(6), *dma(4),
            *dma(chunks), *dma(2), *dma(chunks + 2), *dma(chunks + 2),
            *dma(chunks), *dma(3 * chunks), *dma(chunks), *dma(3 * chunks),
        ],
        compiler_params=pltpu.CompilerParams(
            collective_id=0, has_side_effects=True, vmem_limit_bytes=VMEM_LIMIT * MIB
        ),
    )(views_data[0], start, psf_table, psf_index)
    return pl.pallas_call(
        output_kernel,
        grid=(planes // 4,),
        out_shape=jax.ShapeDtypeStruct(start.shape, f32),
        in_specs=[VMEM],
        out_specs=pl.BlockSpec((4, width_x, width_y), lambda i: (i, 0, 0)),
        compiler_params=pltpu.CompilerParams(vmem_limit_bytes=12 * MIB),
    )(gathered.reshape(width_y * planes, width_x))


def solution(mesh):
    return jax.shard_map(
        functools.partial(on_device, mesh.shape["gz"] // 2),
        mesh=mesh,
        in_specs=(P("view", "gz", None, None), P("gz", None, None), P(), P("view")),
        out_specs=P("gz", None, None),
        check_vma=False,
    )
```

time: 176 us -> 121 us (0.69)
  Pallas kernels: 162 us -> 117 us
  local copies, waits for them, and re-layouts: 10.5 us -> 3.2 us
    pallas_call x6 -> x2, Pallas kernels: 162 us -> 117 us  [the longest x1 114 us: on_device(): pl.pallas_call(functools.partial(whole_kernel, blocks, rows), out_shape=j...]
    unnamed x12 -> x3, local copies, waits for them, and re-layouts: 10.5 us -> 3.2 us
where the time goes in v2:
time: 121 us; the launch traced here: 120 us
  Pallas kernels  117 us (97%)
  local copies, waits for them, and re-layouts  3.2 us (3%)
    pallas_call x1, Pallas kernels, on_device(): pl.pallas_call(functools.partial(whole_kernel, blocks, rows), out_shape=j...  114 us
    unnamed x3, local copies, waits for them, and re-layouts  3.2 us
    pallas_call x1, Pallas kernels, on_device(): pl.pallas_call(output_kernel, grid=(planes // 4,), out_shape=jax.ShapeDty...  2.89 us

profile of v2, /device:TPU:17, one launch (start us, length us, event | category | flops | bytes accessed | tf_op | source)
XLA Modules:
  0.0 120.5 jit_solution(4070790753337838611)
XLA Ops:
  0.7 1.3 %copy.5.table_ref = f32[8,3,17]{2,1,0:T(4,128)} copy(f32[8,3,17]{2,0,1:T(8,128)} %param.6) | data formatting | bytes 3264 | tf_op args[2]
  2.0 113.7 %shard_map.46 = f32[384,16,128]{2,1,0:T(8,128)} custom-call(f32[16,128,384]{2,1,0:T(8,128)} %bitcast.3, f32[16,128,384]{2,1,0:T(8,128)} %start_hbm.1, f32[8,3,17]{2,1,0:T(4,128)} %copy.5.table_ref, s32[1]{0:T(128)S(6)} %copy.6.index_ref), custom_call_target="tpu_custom_call" | custom-call | tf_op jit(solution)/shard_map/pallas_call | solution.py:555
  115.7 0.0 copy-start
  115.7 1.9 %copy-done = f32[384,16,128]{2,1,0:T(8,128)S(1)} copy-done((f32[384,16,128]{2,1,0:T(8,128)S(1)}, f32[384,16,128]{2,1,0:T(8,128)}, u32[]{:S(2)}) %copy-start) | copy-done | bytes 3145752
  117.6 2.9 %shard_map.47 = f32[16,128,384]{2,1,0:T(8,128)} custom-call(f32[6144,128]{1,0:T(8,128)S(1)} %bitcast.2), custom_call_target="tpu_custom_call" | custom-call | tf_op jit(solution)/shard_map/pallas_call | solution.py:589
Async XLA Ops:
  115.7 1.9 %copy-start = (f32[384,16,128]{2,1,0:T(8,128)S(1)}, f32[384,16,128]{2,1,0:T(8,128)}, u32[]{:S(2)}) copy-start(f32[384,16,128]{2,1,0:T(8,128)} %shard_map.46) | copy-start | bytes 9437188

commit v3 on v2

--- a/solution.py
+++ b/solution.py
@@ -11,7 +11,7 @@
 MESH = pl.DeviceIdType.MESH
 VMEM = pl.BlockSpec(memory_space=pltpu.VMEM)
 HBM = pl.BlockSpec(memory_space=pltpu.HBM)
-VMEM_LIMIT = 56
+VMEM_LIMIT = 48
 MIB = 1024 * 1024
 
 
@@ -192,9 +192,9 @@
         product_ref[base + i] = piece
 
 
-def whole_kernel(blocks, strip_rows, data_hbm, start_hbm, table_ref, index_ref,
+def whole_kernel(blocks, strip_rows, data_hbm, start_hbm, table_hbm, index_ref,
                  all_ref,
-                 sbuf, dbuf, ts_ref, td_ref, kern_ref, est_ref, est2_ref, data_ref,
+                 sbuf, dbuf, table_ref, ts_ref, td_ref, kern_ref, est_ref, est2_ref, data_ref,
                  lz_ref, x_ref, ly_ref, lyb_ref, xb_ref, lzb_ref, t_ref, s_ref,
                  product_ref, other_ref, other2_ref,
                  load_sem, kern_s, kern_r, e_s, e_r, d_s, d_r, h_s, h_r,
@@ -213,46 +213,56 @@
     k, a, b, c, strip = here.k, here.a, here.b, here.c, here.strip
     below, above = k > 0, k < blocks - 1
     unless = lambda condition: pl.when(jnp.logical_not(condition))
-    load_start = pltpu.make_async_copy(start_hbm, sbuf, load_sem.at[0])
-    load_data = pltpu.make_async_copy(data_hbm, dbuf, load_sem.at[1])
-    load_start.start()
-    load_data.start()
+    pieces = planes // pad
+    loads = []
+    for i, (source, target) in enumerate(((start_hbm, sbuf), (data_hbm, dbuf))):
+        for piece in range(pieces):
+            at = pl.ds(pad * piece, pad)
+            load = pltpu.make_async_copy(source.at[at], target.at[at], load_sem.at[pieces * i + piece])
+            load.start()
+            loads.append(load)
+    load_table = pltpu.make_async_copy(table_hbm, table_ref, load_sem.at[2 * pieces])
+    load_table.start()
     ts3 = ts_ref.reshape(width_y + 2 * reach, stride, width_x)
-
+    greet(here)
+
+    ts_ref[pl.ds(0, reach * stride)] = jnp.zeros((reach * stride, width_x), jnp.float32)
+    ts_ref[pl.ds((width_y + reach) * stride, reach * stride)] = jnp.zeros((reach * stride, width_x), jnp.float32)
+    mine = pl.multiple_of(reach + planes * b, 8)
+    theirs = pl.multiple_of(reach + planes * (1 - b), 8)
+    rows_c = pl.ds(half * c, half)
+    e_copies = []
+    for piece in range(pieces):
+        loads[piece].wait()
+
+        @pl.loop(0, pad, unroll=4)
+        def _(z):
+            ts_ref[pl.ds(reach * stride + pad * piece + z, width_y, stride=stride)] = sbuf[pad * piece + z].T
+
+        e_copy = remote(
+            ts3.at[pl.ds(rows * here.strip_of(a, 1 - b) + half * c, half), pl.ds(pad * piece, pad)],
+            est_ref.at[rows_c, pl.ds(mine + pad * piece, pad)], (e_s, e_r), 6 + piece, here.device(b=1 - b),
+        )
+        e_copy.start()
+        e_copies.append(e_copy)
+
+    load_table.wait()
     table = table_ref[...]
-    kern = jnp.zeros(table.shape[1:], jnp.float32)
-    for i in range(table.shape[0]):
-        kern = jnp.where(index_ref[0] == i, table[i], kern)
+    chosen = lax.broadcasted_iota(jnp.int32, table.shape, 1) == index_ref[0]
+    kern = jnp.sum(jnp.where(chosen, table, 0.0), axis=1)
     kern = kern / jnp.sum(kern, axis=-1, keepdims=True)
     kern_ref[a] = jnp.zeros(kern_ref.shape[1:], jnp.float32)
     kern_ref[a, pl.ds(0, 3), pl.ds(0, taps)] = kern
-    ts_ref[pl.ds(0, reach * stride)] = jnp.zeros((reach * stride, width_x), jnp.float32)
-    ts_ref[pl.ds((width_y + reach) * stride, reach * stride)] = jnp.zeros((reach * stride, width_x), jnp.float32)
+    kern_copy = remote(kern_ref.at[a], kern_ref.at[a], (kern_s, kern_r), 0, here.device(a=1 - a))
+    kern_copy.start()
+
     for z in range(planes):
         td_ref[z, pl.ds(0, pad)] = jnp.zeros((pad, width_x), jnp.float32)
         td_ref[z, pl.ds(pad + width_y, pad)] = jnp.zeros((pad, width_x), jnp.float32)
-    greet(here)
-
-    load_start.wait()
-
-    @pl.loop(0, planes)
-    def _(z):
-        ts_ref[pl.ds(reach * stride + z, width_y, stride=stride)] = sbuf[z].T
-
-    mine = pl.multiple_of(reach + planes * b, 8)
-    theirs = pl.multiple_of(reach + planes * (1 - b), 8)
-    rows_c = pl.ds(half * c, half)
-    e_copy = remote(
-        ts3.at[pl.ds(rows * here.strip_of(a, 1 - b) + half * c, half), pl.ds(0, planes)],
-        est_ref.at[rows_c, pl.ds(mine, planes)], (e_s, e_r), 0, here.device(b=1 - b),
-    )
-    e_copy.start()
-    kern_copy = remote(kern_ref.at[a], kern_ref.at[a], (kern_s, kern_r), 0, here.device(a=1 - a))
-    kern_copy.start()
-
-    load_data.wait()
-
-    @pl.loop(0, planes)
+    for load in loads[pieces:]:
+        load.wait()
+
+    @pl.loop(0, planes, unroll=4)
     def _(z):
         td_ref[z, pl.ds(pad, width_y)] = dbuf[z].T
 
@@ -267,16 +277,16 @@
             copy.start()
             d_copies.append(copy)
 
-    @pl.loop(0, wide)
+    @pl.loop(0, wide, unroll=8)
     def _(row):
         est_ref[row, pl.ds(mine, planes)] = ts3[rows * strip + row, pl.ds(0, planes)]
 
-    @pl.loop(0, planes)
+    @pl.loop(0, planes, unroll=2)
     def _(z):
         data_ref[a, pad + planes * b + z] = td_ref[z, pl.ds(pl.multiple_of(rows * strip, 8), tall)]
 
     def zero(ref, first_row, count, first, size):
-        @pl.loop(0, count)
+        @pl.loop(0, count, unroll=8)
         def _(row):
             ref[first_row + row, pl.ds(first, size)] = jnp.zeros((size, width_x), jnp.float32)
 
@@ -302,7 +312,8 @@
     kern_copy.wait()
     write_matrices(kern_ref, taps, (lz_ref, x_ref, ly_ref, lyb_ref, xb_ref, lzb_ref))
 
-    e_copy.wait()
+    for copy in e_copies:
+        copy.wait()
     relay = remote(
         est_ref.at[rows_c, pl.ds(theirs, planes)], est_ref.at[rows_c, pl.ds(theirs, planes)],
         (e_s, e_r), 1, here.partner(),
@@ -384,8 +395,8 @@
         back_rows(reach * q, reach, lzb_ref, s_ref, product_ref)
         swap(q).start()
 
-    unless(left)(lambda: zero(est2_ref, 0, reach, reach, depth))
-    unless(right)(lambda: zero(est2_ref, reach + rows, reach, reach, depth))
+    unless(left)(lambda: zero(est2_ref, 0, reach, 0, depth + 2 * reach))
+    unless(right)(lambda: zero(est2_ref, reach + rows, reach, 0, depth + 2 * reach))
     unless(below)(lambda: zero(est2_ref, 0, wide, 0, reach))
     unless(above)(lambda: zero(est2_ref, 0, wide, reach + depth, reach))
 
@@ -424,7 +435,7 @@
         q = e - 1
         swap(q).wait_recv()
 
-        @pl.loop(0, reach)
+        @pl.loop(0, reach, unroll=4)
         def _(r):
             row = reach * q + r
             factor = root(product_ref[row] * other_ref[row])
@@ -434,24 +445,43 @@
         pl.when((i == 1) & right)(to_right.start)
         pl.when(z_sends)(along_z(e).start)
 
-    pl.when(left)(to_right.wait_recv)
-    pl.when(right)(to_left.wait_recv)
-    pl.when(z_sends)(along_z(0).start)
-    pl.when(z_sends)(along_z(chunks + 1).start)
+    zone = pl.ds(z_to, reach)
+    corner_left = remote(
+        est2_ref.at[pl.ds(reach, reach), zone], est2_ref.at[pl.ds(reach + rows, reach), zone],
+        (y_s, y_r), 2, here.of_strip(strip - 1),
+    )
+    corner_right = remote(
+        est2_ref.at[pl.ds(rows, reach), zone], est2_ref.at[pl.ds(0, reach), zone],
+        (y_s, y_r), 3, here.of_strip(strip + 1),
+    )
+
+    def exists(e):
+        return ((e > 0) | left) & ((e < chunks + 1) | right)
 
     @pl.loop(0, chunks + 3)
     def _(i):
-        @pl.when((i < chunks + 2) & z_gets)
+        e = chunk_of(i)
+
+        @pl.when((i < chunks) & z_gets)
         def _():
-            e = chunk_of(i)
             along_z(e).wait_recv()
-            across(e).start()
+            pl.when((i == 0) & left)(corner_left.start)
+            pl.when((i == 1) & right)(corner_right.start)
+
+        pl.when((i == chunks) & z_gets & left)(corner_right.wait_recv)
+        pl.when((i == chunks + 1) & z_gets & right)(corner_left.wait_recv)
+        pl.when((i < chunks + 2) & z_gets & exists(e))(across(e).start)
+
+        @pl.when(i == chunks + 1)
+        def _():
+            pl.when(left)(to_right.wait_recv)
+            pl.when(right)(to_left.wait_recv)
 
         @pl.when(i >= 1)
         def _():
-            e = chunk_of(i - 1)
-            pl.when(q_gets)(across(e).wait_recv)
-            forward_rows(reach * e, reach, est2_ref, lz_ref, x_ref, t_ref)
+            before = chunk_of(i - 1)
+            pl.when(q_gets & exists(before))(across(before).wait_recv)
+            forward_rows(reach * before, reach, est2_ref, lz_ref, x_ref, t_ref)
 
     @pl.loop(0, chunks)
     def _(q):
@@ -494,7 +524,7 @@
     def _(q):
         last_swap(q).wait_recv()
 
-        @pl.loop(0, part)
+        @pl.loop(0, part, unroll=4)
         def _(r):
             row = reach * q + part * c + r
             factor = root(product_ref[row] * other2_ref[row])
@@ -526,10 +556,13 @@
     pl.when(left)(to_left.wait_send)
     pl.when(right)(to_right.wait_send)
 
+    pl.when(left & z_gets)(corner_left.wait_send)
+    pl.when(right & z_gets)(corner_right.wait_send)
+
     @pl.loop(0, chunks + 2)
     def _(e):
-        pl.when(z_sends)(along_z(e).wait_send)
-        pl.when(z_gets)(across(e).wait_send)
+        pl.when((e > 0) & (e < chunks + 1) & z_sends)(along_z(e).wait_send)
+        pl.when(z_gets & exists(e))(across(e).wait_send)
 
 
 def output_kernel(all_ref, out_ref):
@@ -552,14 +585,16 @@
     chunks = rows // reach
     dma = lambda n: [pltpu.SemaphoreType.DMA((n,)), pltpu.SemaphoreType.DMA((n,))]
 
+    by_row = jnp.transpose(psf_table, (1, 0, 2))
     gathered = pl.pallas_call(
         functools.partial(whole_kernel, blocks, rows),
         out_shape=jax.ShapeDtypeStruct((width_y, planes, width_x), f32),
-        in_specs=[HBM, HBM, VMEM, pl.BlockSpec(memory_space=pltpu.SMEM)],
+        in_specs=[HBM, HBM, HBM, pl.BlockSpec(memory_space=pltpu.SMEM)],
         out_specs=VMEM,
         scratch_shapes=[
             pltpu.VMEM(start.shape, f32),
             pltpu.VMEM(start.shape, f32),
+            pltpu.VMEM(by_row.shape, f32),
             pltpu.VMEM(((width_y + 2 * reach) * odd_stride(planes), width_x), f32),
             pltpu.VMEM((planes, width_y + 2 * pad, width_x), f32),
             pltpu.VMEM((2, 8, 128), f32),
@@ -577,15 +612,15 @@
             pltpu.VMEM((rows, depth, width_x), f32),
             pltpu.VMEM((rows, depth, width_x), f32),
             pltpu.VMEM((rows, depth, width_x), f32),
-            pltpu.SemaphoreType.DMA((2,)),
-            *dma(1), *dma(6), *dma(6), *dma(4),
-            *dma(chunks), *dma(2), *dma(chunks + 2), *dma(chunks + 2),
+            pltpu.SemaphoreType.DMA((2 * (planes // pad) + 1,)),
+            *dma(1), *dma(6 + planes // pad), *dma(6), *dma(4),
+            *dma(chunks), *dma(4), *dma(chunks + 2), *dma(chunks + 2),
             *dma(chunks), *dma(3 * chunks), *dma(chunks), *dma(3 * chunks),
         ],
         compiler_params=pltpu.CompilerParams(
             collective_id=0, has_side_effects=True, vmem_limit_bytes=VMEM_LIMIT * MIB
         ),
-    )(views_data[0], start, psf_table, psf_index)
+    )(views_data[0], start, by_row, psf_index)
     return pl.pallas_call(
         output_kernel,
         grid=(planes // 4,),

time: 121 us -> 114 us (0.942)
  Pallas kernels: 117 us -> 111 us
  local copies, waits for them, and re-layouts: 3.2 us -> 0.7 us
    pallas_call x1, Pallas kernels: 114 us -> 108 us  [on_device(): pl.pallas_call(functools.partial(whole_kernel, blocks, rows), out_shape=j...]
    unnamed x3 -> x2, local copies, waits for them, and re-layouts: 3.2 us -> 0.7 us
where the time goes in v3:
time: 114 us; the launch traced here: 112 us
  Pallas kernels  111 us (97%)
    pallas_call x1, Pallas kernels, on_device(): pl.pallas_call(functools.partial(whole_kernel, blocks, rows), out_shape=j...  108 us
    pallas_call x1, Pallas kernels, on_device(): pl.pallas_call(output_kernel, grid=(planes // 4,), out_shape=jax.ShapeDty...  2.92 us

profile of v3, /device:TPU:17, one launch (start us, length us, event | category | flops | bytes accessed | tf_op | source)
XLA Modules:
  0.0 112.4 jit_solution(18131708403563540695)
XLA Ops:
  0.7 0.0 copy-start
  0.7 0.7 copy-done
  1.4 108.1 %shard_map.46 = f32[384,16,128]{2,1,0:T(8,128)S(1)} custom-call(f32[16,128,384]{2,1,0:T(8,128)} %bitcast.5, f32[16,128,384]{2,1,0:T(8,128)} %start_hbm.1, f32[3,8,17]{2,1,0:T(8,128)S(1)} %bitcast.4, s32[1]{0:T(128)S(6)} %copy.5.index_ref), custom_call_target="tpu_custom_call" | custom-call | tf_op jit(solution)/shard_map/pallas_call | solution.py:589
  109.5 2.9 %shard_map.47 = f32[16,128,384]{2,1,0:T(8,128)} custom-call(f32[6144,128]{1,0:T(8,128)S(1)} %bitcast.3), custom_call_target="tpu_custom_call" | custom-call | tf_op jit(solution)/shard_map/pallas_call | solution.py:624
Async XLA Ops:
  0.7 0.7 copy-start

commit v4 on v3

v4 whole, which is shorter than its diff:
```python
import functools
import jax
import jax.numpy as jnp
from jax import lax
from jax.experimental import pallas as pl
from jax.experimental.pallas import tpu as pltpu
from jax.sharding import PartitionSpec as P

ITERS = 2
GROUP = 32
MESH = pl.DeviceIdType.MESH
VMEM = pl.BlockSpec(memory_space=pltpu.VMEM)
HBM = pl.BlockSpec(memory_space=pltpu.HBM)
VMEM_LIMIT = 48
MIB = 1024 * 1024


def split(value):
    high = value.astype(jnp.bfloat16)
    return high, (value - high.astype(jnp.float32)).astype(jnp.bfloat16)


def dot(lhs, rhs):
    return jnp.dot(lhs, rhs, preferred_element_type=jnp.float32)


def odd_stride(rows):
    return rows + 8 if (rows // 8) % 2 == 0 else rows


class Place:
    def __init__(self, blocks):
        view, gz = lax.axis_index("view"), lax.axis_index("gz")
        self.blocks = blocks
        self.a, self.c = view // 2, view % 2
        self.k, self.b = gz // 2, gz % 2
        self.strip = self.strip_of(self.a, self.b)

    @staticmethod
    def strip_of(a, b):
        return 2 * a + (a + b) % 2

    def device(self, a=None, c=None, k=None, b=None):
        a = self.a if a is None else a
        c = self.c if c is None else c
        k = self.k if k is None else k
        b = self.b if b is None else b
        return (2 * a + c, 2 * k + b)

    def of_strip(self, strip):
        return self.device(a=strip // 2, b=(strip % 2 + strip // 2) % 2)

    def partner(self):
        return self.device(c=1 - self.c)

    def others(self):
        a, b = self.a, self.b
        return ((a, 1 - b), (1 - a, b), (1 - a, 1 - b))


def remote(src, dst, sems, index, device):
    send, recv = sems
    return pltpu.make_async_remote_copy(
        src_ref=src, dst_ref=dst, send_sem=send.at[index], recv_sem=recv.at[index],
        device_id=device, device_id_type=MESH,
    )


def greet(here):
    barrier = pltpu.get_barrier_semaphore()

    def signal(device):
        pl.semaphore_signal(barrier, inc=1, device_id=device, device_id_type=MESH)

    signal(here.partner())
    count = 1
    for a, b in here.others():
        signal(here.device(a=a, b=b))
        count += 1
    for step in (-1, 1):
        there = here.k + step
        inside = (there >= 0) & (there < here.blocks)
        pl.when(inside)(functools.partial(lambda there: signal(here.device(k=there)), there))
        count = count + inside.astype(jnp.int32)
    pl.semaphore_wait(barrier, count)


def band(taps, outputs, inputs, sign, shift):
    at = sign * (
        lax.broadcasted_iota(jnp.int32, (outputs, inputs), 1)
        - lax.broadcasted_iota(jnp.int32, (outputs, inputs), 0)
    ) + shift
    total = jnp.zeros((outputs, inputs), jnp.float32)
    for tap, value in enumerate(taps):
        total = jnp.where(at == tap, value, total)
    return total


def write_left(ref, index, matrix):
    high, low = split(matrix)
    rows, depth = matrix.shape
    top = jnp.concatenate([high, high], axis=1)
    bottom = jnp.concatenate([low, low], axis=1)
    ref[index] = jnp.concatenate([top, bottom], axis=0)


def write_right(ref, index, matrix):
    high, low = split(matrix)
    half = jnp.concatenate([high, low], axis=1)
    ref[index] = jnp.concatenate([half, half], axis=0)


def write_matrices(kern_ref, taps, refs):
    lz_ref, x_ref, ly_ref, lyb_ref, xb_ref, lzb_ref = refs
    reach = taps - 1
    pad = reach // 2
    for which in range(2):
        rows = kern_ref[which]
        kz, kx, ky = ([rows[r:r + 1, t:t + 1] for t in range(taps)] for r in range(3))
        outputs, inputs = lz_ref.shape[1] // 2, lz_ref.shape[2] // 2
        write_left(lz_ref, which, band(kz, outputs, inputs, 1, 0))
        write_right(x_ref, which, band(kx, x_ref.shape[1] // 2, x_ref.shape[2] // 2, -1, pad))
        write_left(ly_ref, which, band(ky, ly_ref.shape[1] // 2, ly_ref.shape[2] // 2, 1, 0))
        write_left(lyb_ref, which, band(ky, lyb_ref.shape[1] // 2, lyb_ref.shape[2] // 2, -1, reach))
        write_right(xb_ref, which, band(kx, xb_ref.shape[1] // 2, xb_ref.shape[2] // 2, 1, pad))
        write_left(lzb_ref, which, band(kz, lzb_ref.shape[1] // 2, lzb_ref.shape[2] // 2, -1, reach))


def sides(product):
    half = product.shape[1] // 2
    return product[:, :half] + product[:, half:]


def stack(product):
    half = product.shape[0] // 2
    return product[:half] + product[half:]


def cut(value, count):
    lanes = value.shape[1] // count
    return [value[:, i * lanes:(i + 1) * lanes] for i in range(count)]


def stacked(values):
    return jnp.concatenate([jnp.concatenate(split(value), axis=0) for value in values], axis=1)


def beside(pieces):
    return jnp.concatenate(split(jnp.concatenate(pieces, axis=0)), axis=1)


def root(value):
    return jnp.sqrt(jnp.sqrt(value))


def forward_rows(base, count, est_ref, lz_ref, x_ref, t_ref):
    outer = lz_ref.shape[1] // 2
    half = t_ref.shape[0] // 2
    stride = half // est_ref.shape[0]
    left = lz_ref[...].reshape(4 * outer, lz_ref.shape[2])
    both = dot(left, stacked([est_ref[base + i] for i in range(count)]))
    for which in range(2):
        along_z = stack(both[2 * outer * which:2 * outer * (which + 1)])
        along_x = sides(dot(beside(cut(along_z, count)), x_ref[which]))
        for i in range(count):
            at = pl.multiple_of(half * which + (base + i) * stride, 8)
            t_ref[pl.ds(at, outer)] = along_x[i * outer:(i + 1) * outer]


def ratio_planes(row, planes, wide, data_ref, ly_ref, lyb_ref, xb_ref, t_ref, s_ref):
    count = len(planes)
    reads, tall, rows = ly_ref.shape[2] // 2, ly_ref.shape[1] // 2, lyb_ref.shape[1] // 2
    half = t_ref.shape[0] // 2
    t_stride = half // wide
    s_stride = s_ref.shape[1] // data_ref.shape[1]
    for which in range(2):
        first = half * which + row * t_stride
        right = stacked([t_ref[pl.ds(first + plane, reads, stride=t_stride)] for plane in planes])
        blurred = stack(dot(ly_ref[which], right))
        data = jnp.concatenate([data_ref[which, plane, pl.ds(row, tall)] for plane in planes], axis=1)
        right = jnp.concatenate(split(data / blurred), axis=0)
        along_y = stack(dot(lyb_ref[which], right))
        along_x = sides(dot(beside(cut(along_y, count)), xb_ref[which]))
        for i, plane in enumerate(planes):
            at = pl.multiple_of(plane * s_stride + row, 8)
            s_ref[which, pl.ds(at, rows)] = along_x[i * rows:(i + 1) * rows]


def back_rows(base, count, lzb_ref, s_ref, product_ref):
    outer = lzb_ref.shape[2] // 2
    stride = s_ref.shape[1] // outer
    both = []
    for which in range(2):
        right = stacked([s_ref[which, pl.ds(base + i, outer, stride=stride)] for i in range(count)])
        both.append(stack(dot(lzb_ref[which], right)))
    for i, piece in enumerate(cut(both[0] * both[1], count)):
        product_ref[base + i] = piece


def whole_kernel(blocks, strip_rows, data_hbm, start_hbm, table_hbm, index_ref,
                 all_ref,
                 sbuf, table_ref, td_ref, kern_ref, est_ref, est2_ref, data_ref,
                 lz_ref, x_ref, ly_ref, lyb_ref, xb_ref, lzb_ref, t_ref, t2_ref, s_ref,
                 product_ref, other_ref, other2_ref,
                 load_sem, kern_s, kern_r, e_s, e_r, d_s, d_r, h_s, h_r,
                 p_s, p_r, y_s, y_r, z_s, z_r, q_s, q_r, f_s, f_r, g_s, g_r, o_s, o_r, w_s, w_r):
    here = Place(blocks)
    planes, width_x, width_y = start_hbm.shape
    taps = table_ref.shape[2]
    reach = taps - 1
    pad = reach // 2
    depth = 2 * planes
    rows = strip_rows
    wide = rows + 2 * reach
    tall = rows + 2 * pad
    stride = odd_stride(planes)
    half = wide // 2
    k, a, b, c, strip = here.k, here.a, here.b, here.c, here.strip
    below, above = k > 0, k < blocks - 1
    unless = lambda condition: pl.when(jnp.logical_not(condition))
    pieces = planes // pad

    def load(source, index, piece):
        at = pl.ds(pad * piece, pad)
        copy = pltpu.make_async_copy(source.at[at], sbuf.at[at], load_sem.at[pieces * index + piece])
        copy.start()
        return copy

    loads = [load(start_hbm, 0, piece) for piece in range(pieces)]
    ts_ref = t2_ref.at[pl.ds(0, (width_y + 2 * reach) * stride)]
    load_table = pltpu.make_async_copy(table_hbm, table_ref, load_sem.at[2 * pieces])
    load_table.start()
    ts3 = ts_ref.reshape(width_y + 2 * reach, stride, width_x)
    greet(here)

    ts_ref[pl.ds(0, reach * stride)] = jnp.zeros((reach * stride, width_x), jnp.float32)
    ts_ref[pl.ds((width_y + reach) * stride, reach * stride)] = jnp.zeros((reach * stride, width_x), jnp.float32)
    mine = pl.multiple_of(reach + planes * b, 8)
    theirs = pl.multiple_of(reach + planes * (1 - b), 8)
    rows_c = pl.ds(half * c, half)
    e_copies = []
    for piece in range(pieces):
        loads[piece].wait()

        @pl.loop(0, pad, unroll=4)
        def _(z):
            ts_ref[pl.ds(reach * stride + pad * piece + z, width_y, stride=stride)] = sbuf[pad * piece + z].T

        e_copy = remote(
            ts3.at[pl.ds(rows * here.strip_of(a, 1 - b) + half * c, half), pl.ds(pad * piece, pad)],
            est_ref.at[rows_c, pl.ds(mine + pad * piece, pad)], (e_s, e_r), 6 + piece, here.device(b=1 - b),
        )
        e_copy.start()
        e_copies.append(e_copy)
        loads.append(load(data_hbm, 1, piece))

    load_table.wait()
    table = table_ref[...]
    chosen = lax.broadcasted_iota(jnp.int32, table.shape, 1) == index_ref[0]
    kern = jnp.sum(jnp.where(chosen, table, 0.0), axis=1)
    kern = kern / jnp.sum(kern, axis=-1, keepdims=True)
    kern_ref[a] = jnp.zeros(kern_ref.shape[1:], jnp.float32)
    kern_ref[a, pl.ds(0, 3), pl.ds(0, taps)] = kern
    kern_copy = remote(kern_ref.at[a], kern_ref.at[a], (kern_s, kern_r), 0, here.device(a=1 - a))
    kern_copy.start()

    for z in range(planes):
        td_ref[z, pl.ds(0, pad)] = jnp.zeros((pad, width_x), jnp.float32)
        td_ref[z, pl.ds(pad + width_y, pad)] = jnp.zeros((pad, width_x), jnp.float32)
    for load in loads[pieces:]:
        load.wait()

    @pl.loop(0, planes, unroll=4)
    def _(z):
        td_ref[z, pl.ds(pad, width_y)] = sbuf[z].T

    size = 2 * reach
    parts = rows // size
    chunks = rows // reach
    ascends = lambda strip: strip % 2 == 0

    def new_rows(part, strip):
        first = size * part + (2 * pad if part else 0)
        count = size if part else size + 2 * pad
        return pl.ds(pl.multiple_of(jnp.where(ascends(strip), first, tall - first - count), 8), count)

    def data_copy(part, inner, kind):
        oa, ob = here.others()[kind]
        first, count = ((1 - b) * pad, planes - pad) if inner else (b * (planes - pad), pad)
        target = here.strip_of(oa, ob)
        at = new_rows(part, target)
        return remote(
            td_ref.at[pl.ds(first, count), pl.ds(pl.multiple_of(rows * target + at.start, 8), at.size)],
            data_ref.at[a, pl.ds(pad + planes * b + first, count), at],
            (d_s, d_r), (2 * part + inner) * 3 + kind, here.device(a=oa, b=ob),
        )

    every_data = [(part, inner, kind) for part in range(parts) for inner in range(2) for kind in (2, 0, 1)]
    for which in every_data:
        data_copy(*which).start()

    @pl.loop(0, wide, unroll=8)
    def _(row):
        est_ref[row, pl.ds(mine, planes)] = ts3[rows * strip + row, pl.ds(0, planes)]

    @pl.loop(0, planes, unroll=2)
    def _(z):
        data_ref[a, pad + planes * b + z] = td_ref[z, pl.ds(pl.multiple_of(rows * strip, 8), tall)]

    def zero(ref, first_row, count, first, size):
        @pl.loop(0, count, unroll=8)
        def _(row):
            ref[first_row + row, pl.ds(first, size)] = jnp.zeros((size, width_x), jnp.float32)

    unless(below)(lambda: zero(est_ref, 0, wide, 0, reach))
    unless(above)(lambda: zero(est_ref, 0, wide, reach + depth, reach))

    quad = (*here.others(), (a, b))

    def halo_goes(kind):
        to = k + 2 * quad[kind][1] - 1
        return (to >= 0) & (to < blocks)

    def halo_comes(kind):
        source = k + 1 - 2 * quad[kind][1]
        return (source >= 0) & (source < blocks)

    def halo_copy(part, kind):
        oa, ob = quad[kind]
        at = new_rows(part, strip)
        return remote(
            data_ref.at[oa, pl.ds(pad + ob * (depth - pad), pad), at],
            data_ref.at[oa, pl.ds((1 - ob) * (depth + pad), pad), at],
            (h_s, h_r), 4 * part + kind, here.device(k=k + 2 * ob - 1),
        )

    for kind, (oa, ob) in enumerate(quad):
        unless(halo_comes(kind))(functools.partial(zero, data_ref.at[oa], (1 - ob) * (depth + pad), pad, 0, tall))
    for part in range(parts):
        pl.when(halo_goes(3))(halo_copy(part, 3).start)

    def edges_come(part):
        for kind in (0, 1, 2):
            data_copy(part, 0, kind).wait_recv()
            pl.when(halo_goes(kind))(halo_copy(part, kind).start)

    def rest_comes(part):
        for kind in (0, 1, 2):
            data_copy(part, 1, kind).wait_recv()
        for kind in range(4):
            pl.when(halo_comes(kind))(halo_copy(part, kind).wait_recv)

    kern_copy.wait()
    write_matrices(kern_ref, taps, (lz_ref, x_ref, ly_ref, lyb_ref, xb_ref, lzb_ref))

    for copy in e_copies:
        copy.wait()
    relay = remote(
        est_ref.at[rows_c, pl.ds(theirs, planes)], est_ref.at[rows_c, pl.ds(theirs, planes)],
        (e_s, e_r), 1, here.partner(),
    )
    bottom, top = pl.ds(0, reach), pl.ds(reach + depth, reach)
    first, last = pl.ds(reach, reach), pl.ds(depth, reach)
    up = remote(est_ref.at[rows_c, last], est_ref.at[rows_c, bottom], (e_s, e_r), 2, here.device(k=k + 1))
    down = remote(est_ref.at[rows_c, first], est_ref.at[rows_c, top], (e_s, e_r), 3, here.device(k=k - 1))
    from_below = remote(est_ref.at[rows_c, bottom], est_ref.at[rows_c, bottom], (e_s, e_r), 4, here.partner())
    from_above = remote(est_ref.at[rows_c, top], est_ref.at[rows_c, top], (e_s, e_r), 5, here.partner())
    pl.when(above)(up.start)
    pl.when(below)(down.start)
    relay.start()
    edges_come(0)

    @pl.when(below)
    def _():
        up.wait_recv()
        from_below.start()

    @pl.when(above)
    def _():
        down.wait_recv()
        from_above.start()

    pl.when(above)(up.wait_send)
    pl.when(below)(down.wait_send)
    relay.wait()
    pl.when(below)(from_below.wait)
    pl.when(above)(from_above.wait)

    left, right = strip > 0, strip < 3

    @pl.loop(0, wide // GROUP)
    def _(step):
        forward_rows(step * GROUP, GROUP, est_ref, lz_ref, x_ref, t_ref)

    chunk_of = lambda i: jnp.where(ascends(strip), i, chunks + 1 - i)
    row_of = lambda i: pl.multiple_of(reach * (chunk_of(i) - 1), reach)
    inside = pl.ds(reach, depth)
    step_first = jnp.where(ascends(strip), -1, 1)
    strip_first, strip_last = strip + step_first, strip - step_first
    has_first = (strip_first >= 0) & (strip_first < 4)
    has_last = (strip_last >= 0) & (strip_last < 4)

    def ratio_part(part, from_ref):
        row = pl.multiple_of(size * jnp.where(ascends(strip), part, parts - 1 - part), size)

        @pl.loop(0, (depth + 2 * pad) // (2 * pad))
        def _(step):
            ratio_planes(
                row, [2 * pad * step + i for i in range(2 * pad)], wide,
                data_ref, ly_ref, lyb_ref, xb_ref, from_ref, s_ref,
            )

    def places(part, body):
        pl.loop(1 + 2 * part, 3 + 2 * part)(body)

    def swap(i):
        at = pl.ds(row_of(i), reach)
        return remote(product_ref.at[at], other_ref.at[at], (p_s, p_r), i, here.partner())

    to_block = k + 1 - 2 * c
    z_sends = (to_block >= 0) & (to_block < blocks)
    z_gets = (k - 1 + 2 * c >= 0) & (k - 1 + 2 * c < blocks)
    q_gets = (k + 1 - 2 * c >= 0) & (k + 1 - 2 * c < blocks)
    z_from = pl.multiple_of(reach + (1 - c) * (depth - reach), 8)
    z_to = pl.multiple_of(c * (reach + depth), 8)

    def along_z(i):
        at = pl.ds(reach + row_of(i), reach)
        return remote(
            est2_ref.at[at, pl.ds(z_from, reach)], est2_ref.at[at, pl.ds(z_to, reach)],
            (z_s, z_r), i, here.device(k=to_block),
        )

    def across(i):
        at = pl.ds(reach + row_of(i), reach)
        return remote(
            est2_ref.at[at, pl.ds(z_to, reach)], est2_ref.at[at, pl.ds(z_to, reach)],
            (q_s, q_r), i, here.partner(),
        )

    def to_strip(last, zone, index):
        place = chunks if last else 1
        return remote(
            est2_ref.at[pl.ds(reach + row_of(place), reach), zone],
            est2_ref.at[pl.ds(pl.multiple_of(
                jnp.where(ascends(strip) == bool(last), 0, reach + rows), reach), reach), zone],
            (y_s, y_r), index, here.of_strip(strip_last if last else strip_first),
        )

    def y_main(last):
        return to_strip(last, inside, last)

    def y_corner(last):
        return to_strip(last, pl.ds(z_to, reach), 2 + last)

    unless(left)(lambda: zero(est2_ref, 0, reach, 0, depth + 2 * reach))
    unless(right)(lambda: zero(est2_ref, reach + rows, reach, 0, depth + 2 * reach))
    unless(below)(lambda: zero(est2_ref, 0, wide, 0, reach))
    unless(above)(lambda: zero(est2_ref, 0, wide, reach + depth, reach))

    def first_update(part):
        ratio_part(part, t_ref)

        def make(i):
            back_rows(row_of(i), reach, lzb_ref, s_ref, product_ref)
            swap(i).start()

        def use(i):
            swap(i).wait_recv()

            @pl.loop(0, reach, unroll=4)
            def _(r):
                row = row_of(i) + r
                factor = root(product_ref[row] * other_ref[row])
                est2_ref[reach + row, inside] = est_ref[reach + row, inside] * factor

            pl.when(z_sends)(along_z(i).start)
            pl.when((i == 1) & has_first)(y_main(0).start)
            pl.when((i == chunks) & has_last)(y_main(1).start)

        places(part, make)
        places(part, use)

    def arrive(i):
        @pl.when(z_gets)
        def _():
            along_z(i).wait_recv()
            pl.when((i == 1) & has_first)(y_corner(0).start)
            pl.when((i == chunks) & has_last)(y_corner(1).start)
            across(i).start()

    def arrive_side(last, there):
        @pl.when(there)
        def _():
            y_main(last).wait_recv()

            @pl.when(z_gets)
            def _():
                y_corner(last).wait_recv()
                across((chunks + 1) * last).start()

    def forward(i):
        there = ((i > 0) | has_first) & ((i < chunks + 1) | has_last)
        pl.when(q_gets & there)(across(i).wait_recv)
        forward_rows(pl.multiple_of(reach * chunk_of(i), reach), reach, est2_ref, lz_ref, x_ref, t2_ref)

    half_rows = reach // 2

    def last_swap(i):
        at = pl.ds(row_of(i) + half_rows * (1 - c), half_rows)
        return remote(product_ref.at[at], other2_ref.at[at], (f_s, f_r), i, here.partner())

    def gather(i, kind):
        oa, ob = here.others()[kind]
        return remote(
            other2_ref.at[pl.ds(row_of(i) + half_rows * c, half_rows), pl.ds(pl.multiple_of(planes * ob, 8), planes)],
            all_ref.at[pl.ds(rows * strip + row_of(i) + half_rows * c, half_rows)],
            (g_s, g_r), 3 * i + kind, here.device(a=oa, b=ob),
        )

    def own(i):
        return remote(
            other2_ref.at[pl.ds(row_of(i) + half_rows * c, half_rows), pl.ds(pl.multiple_of(planes * b, 8), planes)],
            all_ref.at[pl.ds(rows * strip + row_of(i) + half_rows * c, half_rows)],
            (o_s, o_r), i, here.partner(),
        )

    def onward(i, kind):
        theirs = here.strip_of(*here.others()[kind])
        chunk = jnp.where(ascends(theirs), i - 1, chunks - i)
        at = pl.ds(rows * theirs + reach * chunk + half_rows * c, half_rows)
        return remote(all_ref.at[at], all_ref.at[at], (w_s, w_r), 3 * i + kind, here.partner())

    def last_update(part):
        ratio_part(part, t2_ref)

        def make(i):
            swap(i).wait_send()
            back_rows(row_of(i), reach, lzb_ref, s_ref, product_ref)
            last_swap(i).start()

        def use(i):
            last_swap(i).wait_recv()

            @pl.loop(0, half_rows, unroll=4)
            def _(r):
                row = row_of(i) + half_rows * c + r
                factor = root(product_ref[row] * other2_ref[row])
                other2_ref[row] = est2_ref[reach + row, inside] * factor
                all_ref[rows * strip + row] = other2_ref[row, pl.ds(pl.multiple_of(planes * b, 8), planes)]

            for kind in (2, 0, 1):
                gather(i, kind).start()
            own(i).start()

        places(part, make)
        places(part, use)

    for part in range(parts - 1):
        edges_come(part + 1)
        rest_comes(part)
        first_update(part)
    early = 2 * (parts - 1) - 1
    pl.loop(1, early)(arrive)
    pl.loop(1, early)(forward)
    rest_comes(parts - 1)
    first_update(parts - 1)
    pl.loop(early, chunks - 1)(arrive)
    arrive_side(0, has_first)
    forward(0)
    pl.loop(early, chunks - 1)(forward)
    for part in range(parts - 2):
        last_update(part)
    pl.loop(chunks - 1, chunks + 1)(arrive)
    pl.loop(chunks - 1, chunks + 1)(forward)
    last_update(parts - 2)
    arrive_side(1, has_last)
    forward(chunks + 1)
    last_update(parts - 1)

    @pl.loop(1, chunks + 1)
    def _(i):
        for kind in range(3):
            gather(i, kind).wait_recv()
            onward(i, kind).start()

    @pl.loop(1, chunks + 1)
    def _(i):
        last_swap(i).wait_send()
        own(i).wait()
        for kind in range(3):
            gather(i, kind).wait_send()
            onward(i, kind).wait()
        pl.when(z_sends)(along_z(i).wait_send)

    for which in every_data:
        data_copy(*which).wait_send()
    for part in range(parts):
        for kind in range(4):
            pl.when(halo_goes(kind))(halo_copy(part, kind).wait_send)
    for last, there in enumerate((has_first, has_last)):
        pl.when(there)(y_main(last).wait_send)
        pl.when(there & z_gets)(y_corner(last).wait_send)

    @pl.loop(0, chunks + 2)
    def _(i):
        there = ((i > 0) | has_first) & ((i < chunks + 1) | has_last)
        pl.when(z_gets & there)(across(i).wait_send)


def output_kernel(all_ref, out_ref):
    group, lanes, width = out_ref.shape
    stride = all_ref.shape[0] // width
    base = pl.program_id(0) * group
    for i in range(group):
        out_ref[i] = all_ref[pl.ds(base + i, width, stride=stride)].T


def on_device(blocks, views_data, start, psf_table, psf_index):
    f32, bf16 = jnp.float32, jnp.bfloat16
    planes, width_x, width_y = start.shape
    reach = psf_table.shape[2] - 1
    pad = reach // 2
    rows = width_y // 4
    depth = 2 * planes
    wide, deep = rows + 2 * reach, depth + 2 * reach
    tall, outer = rows + 2 * pad, depth + 2 * pad
    chunks = rows // reach
    size = 2 * reach
    parts = rows // size
    dma = lambda n: [pltpu.SemaphoreType.DMA((n,)), pltpu.SemaphoreType.DMA((n,))]

    by_row = jnp.transpose(psf_table, (1, 0, 2))
    gathered = pl.pallas_call(
        functools.partial(whole_kernel, blocks, rows),
        out_shape=jax.ShapeDtypeStruct((width_y, planes, width_x), f32),
        in_specs=[HBM, HBM, HBM, pl.BlockSpec(memory_space=pltpu.SMEM)],
        out_specs=VMEM,
        scratch_shapes=[
            pltpu.VMEM(start.shape, f32),
            pltpu.VMEM(by_row.shape, f32),
            pltpu.VMEM((planes, width_y + 2 * pad, width_x), f32),
            pltpu.VMEM((2, 8, 128), f32),
            pltpu.VMEM((wide, deep, width_x), f32),
            pltpu.VMEM((wide, deep, width_x), f32),
            pltpu.VMEM((2, outer, tall, width_x), f32),
            pltpu.VMEM((2, 2 * outer, 2 * deep), bf16),
            pltpu.VMEM((2, 2 * width_x, 2 * width_x), bf16),
            pltpu.VMEM((2, 2 * (size + 2 * pad), 2 * (size + 2 * reach)), bf16),
            pltpu.VMEM((2, 2 * size, 2 * (size + 2 * pad)), bf16),
            pltpu.VMEM((2, 2 * width_x, 2 * width_x), bf16),
            pltpu.VMEM((2, 2 * depth, 2 * outer), bf16),
            pltpu.VMEM((2 * wide * odd_stride(outer), width_x), f32),
            pltpu.VMEM((2 * wide * odd_stride(outer), width_x), f32),
            pltpu.VMEM((2, outer * odd_stride(rows), width_x), f32),
            pltpu.VMEM((rows, depth, width_x), f32),
            pltpu.VMEM((rows, depth, width_x), f32),
            pltpu.VMEM((rows, depth, width_x), f32),
            pltpu.SemaphoreType.DMA((2 * (planes // pad) + 1,)),
            *dma(1), *dma(6 + planes // pad), *dma(6 * parts), *dma(4 * parts),
            *dma(chunks + 1), *dma(4), *dma(chunks + 2), *dma(chunks + 2),
            *dma(chunks + 1), *dma(3 * chunks + 3), *dma(chunks + 1), *dma(3 * chunks + 3),
        ],
        compiler_params=pltpu.CompilerParams(
            collective_id=0, has_side_effects=True, vmem_limit_bytes=VMEM_LIMIT * MIB
        ),
    )(views_data[0], start, by_row, psf_index)
    return pl.pallas_call(
        output_kernel,
        grid=(planes // 4,),
        out_shape=jax.ShapeDtypeStruct(start.shape, f32),
        in_specs=[VMEM],
        out_specs=pl.BlockSpec((4, width_x, width_y), lambda i: (i, 0, 0)),
        compiler_params=pltpu.CompilerParams(vmem_limit_bytes=12 * MIB),
    )(gathered.reshape(width_y * planes, width_x))


def solution(mesh):
    return jax.shard_map(
        functools.partial(on_device, mesh.shape["gz"] // 2),
        mesh=mesh,
        in_specs=(P("view", "gz", None, None), P("gz", None, None), P(), P("view")),
        out_specs=P("gz", None, None),
        check_vma=False,
    )
```

time: 114 us -> 111 us (0.974); the launches traced: 112 us -> 111 us
  Pallas kernels: 111 us -> 109 us
    pallas_call x1, Pallas kernels: 108 us -> 106 us  [on_device(): pl.pallas_call(functools.partial(whole_kernel, blocks, rows), out_shape=j...]
where the time goes in v4:
time: 111 us
  Pallas kernels  109 us (98%)
    pallas_call x1, Pallas kernels, on_device(): pl.pallas_call(functools.partial(whole_kernel, blocks, rows), out_shape=j...  106 us
    pallas_call x1, Pallas kernels, on_device(): pl.pallas_call(output_kernel, grid=(planes // 4,), out_shape=jax.ShapeDty...  2.92 us

profile of v4, /device:TPU:17, one launch (start us, length us, event | category | flops | bytes accessed | tf_op | source)
XLA Modules:
  0.0 110.6 jit_solution(7568563041861784214)
XLA Ops:
  0.7 0.0 copy-start
  0.7 0.7 copy-done
  1.4 106.3 %shard_map.46 = f32[384,16,128]{2,1,0:T(8,128)S(1)} custom-call(f32[16,128,384]{2,1,0:T(8,128)} %bitcast.5, f32[16,128,384]{2,1,0:T(8,128)} %start_hbm.1, f32[3,8,17]{2,1,0:T(8,128)S(1)} %bitcast.4, s32[1]{0:T(128)S(6)} %copy.5.index_ref), custom_call_target="tpu_custom_call" | custom-call | tf_op jit(solution)/shard_map/pallas_call | solution.py:634
  107.6 2.9 %shard_map.47 = f32[16,128,384]{2,1,0:T(8,128)} custom-call(f32[6144,128]{1,0:T(8,128)S(1)} %bitcast.3), custom_call_target="tpu_custom_call" | custom-call | tf_op jit(solution)/shard_map/pallas_call | solution.py:668
Async XLA Ops:
  0.7 0.7 copy-start

commit v5 on v4

--- a/solution.py
+++ b/solution.py
@@ -295,7 +295,7 @@
             (d_s, d_r), (2 * part + inner) * 3 + kind, here.device(a=oa, b=ob),
         )
 
-    every_data = [(part, inner, kind) for part in range(parts) for inner in range(2) for kind in (2, 0, 1)]
+    every_data = [(part, inner, kind) for inner in range(2) for part in range(parts) for kind in (2, 0, 1)]
     for which in every_data:
         data_copy(*which).start()
 
@@ -380,12 +380,12 @@
         down.wait_recv()
         from_above.start()
 
+    edges_come(1)
     pl.when(above)(up.wait_send)
     pl.when(below)(down.wait_send)
     relay.wait()
     pl.when(below)(from_below.wait)
     pl.when(above)(from_above.wait)
-
     left, right = strip > 0, strip < 3
 
     @pl.loop(0, wide // GROUP)
@@ -403,12 +403,9 @@
     def ratio_part(part, from_ref):
         row = pl.multiple_of(size * jnp.where(ascends(strip), part, parts - 1 - part), size)
 
-        @pl.loop(0, (depth + 2 * pad) // (2 * pad))
-        def _(step):
-            ratio_planes(
-                row, [2 * pad * step + i for i in range(2 * pad)], wide,
-                data_ref, ly_ref, lyb_ref, xb_ref, from_ref, s_ref,
-            )
+        ratio_planes(
+            row, range(depth + 2 * pad), wide, data_ref, ly_ref, lyb_ref, xb_ref, from_ref, s_ref,
+        )
 
     def places(part, body):
         pl.loop(1 + 2 * part, 3 + 2 * part)(body)
@@ -448,7 +445,14 @@
         )
 
     def y_main(last):
-        return to_strip(last, inside, last)
+        return to_strip(last, pl.ds(pl.multiple_of(reach + planes * c, 8), planes), last)
+
+    def y_across(last):
+        at = pl.ds(reach + row_of((chunks + 1) * last), reach)
+        zone = pl.ds(pl.multiple_of(reach + planes * c, 8), planes)
+        return remote(
+            est2_ref.at[at, zone], est2_ref.at[at, zone], (q_s, q_r), chunks + 2 + last, here.partner(),
+        )
 
     def y_corner(last):
         return to_strip(last, pl.ds(z_to, reach), 2 + last)
@@ -493,11 +497,16 @@
         @pl.when(there)
         def _():
             y_main(last).wait_recv()
+            y_across(last).start()
 
             @pl.when(z_gets)
             def _():
                 y_corner(last).wait_recv()
                 across((chunks + 1) * last).start()
+
+    def side_forward(last, there):
+        pl.when(there)(y_across(last).wait_recv)
+        forward((chunks + 1) * last)
 
     def forward(i):
         there = ((i > 0) | has_first) & ((i < chunks + 1) | has_last)
@@ -531,8 +540,7 @@
         at = pl.ds(rows * theirs + reach * chunk + half_rows * c, half_rows)
         return remote(all_ref.at[at], all_ref.at[at], (w_s, w_r), 3 * i + kind, here.partner())
 
-    def last_update(part):
-        ratio_part(part, t2_ref)
+    def last_update():
 
         def make(i):
             swap(i).wait_send()
@@ -553,30 +561,38 @@
                 gather(i, kind).start()
             own(i).start()
 
-        places(part, make)
-        places(part, use)
-
+        return make, use
+
+    make, use = last_update()
+    for part in range(2, parts):
+        edges_come(part)
+    early = 2 * (parts - 1) - 1
     for part in range(parts - 1):
-        edges_come(part + 1)
         rest_comes(part)
         first_update(part)
-    early = 2 * (parts - 1) - 1
     pl.loop(1, early)(arrive)
     pl.loop(1, early)(forward)
     rest_comes(parts - 1)
     first_update(parts - 1)
     pl.loop(early, chunks - 1)(arrive)
     arrive_side(0, has_first)
-    forward(0)
     pl.loop(early, chunks - 1)(forward)
+    side_forward(0, has_first)
     for part in range(parts - 2):
-        last_update(part)
+        ratio_part(part, t2_ref)
+        places(part, make)
     pl.loop(chunks - 1, chunks + 1)(arrive)
+    for part in range(parts - 2):
+        places(part, use)
     pl.loop(chunks - 1, chunks + 1)(forward)
-    last_update(parts - 2)
+    ratio_part(parts - 2, t2_ref)
+    places(parts - 2, make)
     arrive_side(1, has_last)
-    forward(chunks + 1)
-    last_update(parts - 1)
+    places(parts - 2, use)
+    side_forward(1, has_last)
+    ratio_part(parts - 1, t2_ref)
+    places(parts - 1, make)
+    places(parts - 1, use)
 
     @pl.loop(1, chunks + 1)
     def _(i):
@@ -600,6 +616,7 @@
             pl.when(halo_goes(kind))(halo_copy(part, kind).wait_send)
     for last, there in enumerate((has_first, has_last)):
         pl.when(there)(y_main(last).wait_send)
+        pl.when(there)(y_across(last).wait_send)
         pl.when(there & z_gets)(y_corner(last).wait_send)
 
     @pl.loop(0, chunks + 2)
@@ -658,7 +675,7 @@
             pltpu.VMEM((rows, depth, width_x), f32),
             pltpu.SemaphoreType.DMA((2 * (planes // pad) + 1,)),
             *dma(1), *dma(6 + planes // pad), *dma(6 * parts), *dma(4 * parts),
-            *dma(chunks + 1), *dma(4), *dma(chunks + 2), *dma(chunks + 2),
+            *dma(chunks + 1), *dma(4), *dma(chunks + 1), *dma(chunks + 4),
             *dma(chunks + 1), *dma(3 * chunks + 3), *dma(chunks + 1), *dma(3 * chunks + 3),
         ],
         compiler_params=pltpu.CompilerParams(

time: 111 us -> 101 us (0.910)
  Pallas kernels: 109 us -> 99.2 us
    pallas_call x1, Pallas kernels: 106 us -> 96.3 us  [on_device(): pl.pallas_call(functools.partial(whole_kernel, blocks, rows), out_shape=j...]
where the time goes in v5:
time: 101 us
  Pallas kernels  99.2 us (98%)
    pallas_call x1, Pallas kernels, on_device(): pl.pallas_call(functools.partial(whole_kernel, blocks, rows), out_shape=j...  96.3 us
    pallas_call x1, Pallas kernels, on_device(): pl.pallas_call(output_kernel, grid=(planes // 4,), out_shape=jax.ShapeDty...  2.92 us

profile of v5, /device:TPU:17, one launch (start us, length us, event | category | flops | bytes accessed | tf_op | source)
XLA Modules:
  0.0 100.6 jit_solution(5595412594124515771)
XLA Ops:
  0.7 0.0 copy-start
  0.7 0.7 copy-done
  1.4 96.3 %shard_map.46 = f32[384,16,128]{2,1,0:T(8,128)S(1)} custom-call(f32[16,128,384]{2,1,0:T(8,128)} %bitcast.5, f32[16,128,384]{2,1,0:T(8,128)} %start_hbm.1, f32[3,8,17]{2,1,0:T(8,128)S(1)} %bitcast.4, s32[1]{0:T(128)S(6)} %copy.5.index_ref), custom_call_target="tpu_custom_call" | custom-call | tf_op jit(solution)/shard_map/pallas_call | solution.py:651
  97.6 2.9 %shard_map.47 = f32[16,128,384]{2,1,0:T(8,128)} custom-call(f32[6144,128]{1,0:T(8,128)S(1)} %bitcast.3), custom_call_target="tpu_custom_call" | custom-call | tf_op jit(solution)/shard_map/pallas_call | solution.py:685
Async XLA Ops:
  0.7 0.7 copy-start

commit v6 on v5

--- a/solution.py
+++ b/solution.py
@@ -12,6 +12,7 @@
 VMEM = pl.BlockSpec(memory_space=pltpu.VMEM)
 HBM = pl.BlockSpec(memory_space=pltpu.HBM)
 VMEM_LIMIT = 48
+SEMAPHORES = 25
 MIB = 1024 * 1024
 
 
@@ -26,6 +27,10 @@
 
 def odd_stride(rows):
     return rows + 8 if (rows // 8) % 2 == 0 else rows
+
+
+def part_sizes(chunks):
+    return (chunks - 4, 2, 2)
 
 
 class Place:
@@ -110,8 +115,8 @@
     ref[index] = jnp.concatenate([half, half], axis=0)
 
 
-def write_matrices(kern_ref, taps, refs):
-    lz_ref, x_ref, ly_ref, lyb_ref, xb_ref, lzb_ref = refs
+def write_matrices(kern_ref, taps, refs, y_refs):
+    lz_ref, x_ref, xb_ref, lzb_ref = refs
     reach = taps - 1
     pad = reach // 2
     for which in range(2):
@@ -120,8 +125,8 @@
         outputs, inputs = lz_ref.shape[1] // 2, lz_ref.shape[2] // 2
         write_left(lz_ref, which, band(kz, outputs, inputs, 1, 0))
         write_right(x_ref, which, band(kx, x_ref.shape[1] // 2, x_ref.shape[2] // 2, -1, pad))
-        write_left(ly_ref, which, band(ky, ly_ref.shape[1] // 2, ly_ref.shape[2] // 2, 1, 0))
-        write_left(lyb_ref, which, band(ky, lyb_ref.shape[1] // 2, lyb_ref.shape[2] // 2, -1, reach))
+        for i, ref in enumerate(y_refs):
+            write_left(ref, which, band(ky, ref.shape[1] // 2, ref.shape[2] // 2, *((-1, reach) if i % 2 else (1, 0))))
         write_right(xb_ref, which, band(kx, xb_ref.shape[1] // 2, xb_ref.shape[2] // 2, 1, pad))
         write_left(lzb_ref, which, band(kz, lzb_ref.shape[1] // 2, lzb_ref.shape[2] // 2, -1, reach))
 
@@ -200,10 +205,11 @@
 def whole_kernel(blocks, strip_rows, data_hbm, start_hbm, table_hbm, index_ref,
                  all_ref,
                  sbuf, table_ref, td_ref, kern_ref, est_ref, est2_ref, data_ref,
-                 lz_ref, x_ref, ly_ref, lyb_ref, xb_ref, lzb_ref, t_ref, t2_ref, s_ref,
-                 product_ref, other_ref, other2_ref,
-                 load_sem, kern_s, kern_r, e_s, e_r, d_s, d_r, h_s, h_r,
-                 p_s, p_r, y_s, y_r, z_s, z_r, q_s, q_r, f_s, f_r, g_s, g_r, o_s, o_r, w_s, w_r):
+                 lz_ref, x_ref, xb_ref, lzb_ref, t_ref, t2_ref, s_ref,
+                 product_ref, other_ref, other2_ref, new_ref, *rest):
+    y_refs = rest[:-SEMAPHORES]
+    (load_sem, kern_s, kern_r, e_s, e_r, d_s, d_r, h_s, h_r,
+     p_s, p_r, y_s, y_r, z_s, z_r, q_s, q_r, f_s, f_r, g_s, g_r, o_s, o_r, w_s, w_r) = rest[-SEMAPHORES:]
     here = Place(blocks)
     planes, width_x, width_y = start_hbm.shape
     taps = table_ref.shape[2]
@@ -274,14 +280,15 @@
     def _(z):
         td_ref[z, pl.ds(pad, width_y)] = sbuf[z].T
 
-    size = 2 * reach
-    parts = rows // size
     chunks = rows // reach
+    sizes = part_sizes(chunks)
+    parts = len(sizes)
+    starts = [sum(sizes[:part]) for part in range(parts)]
     ascends = lambda strip: strip % 2 == 0
 
     def new_rows(part, strip):
-        first = size * part + (2 * pad if part else 0)
-        count = size if part else size + 2 * pad
+        first = reach * starts[part] + (2 * pad if part else 0)
+        count = reach * sizes[part] + (0 if part else 2 * pad)
         return pl.ds(pl.multiple_of(jnp.where(ascends(strip), first, tall - first - count), 8), count)
 
     def data_copy(part, inner, kind):
@@ -351,7 +358,7 @@
             pl.when(halo_comes(kind))(halo_copy(part, kind).wait_recv)
 
     kern_copy.wait()
-    write_matrices(kern_ref, taps, (lz_ref, x_ref, ly_ref, lyb_ref, xb_ref, lzb_ref))
+    write_matrices(kern_ref, taps, (lz_ref, x_ref, xb_ref, lzb_ref), y_refs)
 
     for copy in e_copies:
         copy.wait()
@@ -400,15 +407,23 @@
     has_first = (strip_first >= 0) & (strip_first < 4)
     has_last = (strip_last >= 0) & (strip_last < 4)
 
+    def row_of_part(part):
+        before, after = starts[part], chunks - starts[part] - sizes[part]
+        return pl.multiple_of(reach * jnp.where(ascends(strip), before, after), reach)
+
+    def back_part(part):
+        back_rows(row_of_part(part), reach * sizes[part], lzb_ref, s_ref, product_ref)
+
     def ratio_part(part, from_ref):
-        row = pl.multiple_of(size * jnp.where(ascends(strip), part, parts - 1 - part), size)
+        row = row_of_part(part)
+        ly_ref, lyb_ref = y_refs[2 * part], y_refs[2 * part + 1]
 
         ratio_planes(
             row, range(depth + 2 * pad), wide, data_ref, ly_ref, lyb_ref, xb_ref, from_ref, s_ref,
         )
 
     def places(part, body):
-        pl.loop(1 + 2 * part, 3 + 2 * part)(body)
+        pl.loop(1 + starts[part], 1 + starts[part] + sizes[part])(body)
 
     def swap(i):
         at = pl.ds(row_of(i), reach)
@@ -462,11 +477,12 @@
     unless(below)(lambda: zero(est2_ref, 0, wide, 0, reach))
     unless(above)(lambda: zero(est2_ref, 0, wide, reach + depth, reach))
 
+    late = 1 + starts[parts - 1]
+
     def first_update(part):
         ratio_part(part, t_ref)
 
         def make(i):
-            back_rows(row_of(i), reach, lzb_ref, s_ref, product_ref)
             swap(i).start()
 
         def use(i):
@@ -482,8 +498,10 @@
             pl.when((i == 1) & has_first)(y_main(0).start)
             pl.when((i == chunks) & has_last)(y_main(1).start)
 
-        places(part, make)
-        places(part, use)
+        flip = lambda body: (lambda i: body(late + chunks - i)) if part == parts - 1 else body
+        back_part(part)
+        places(part, lambda i: flip(make)(i))
+        places(part, lambda i: flip(use)(i))
 
     def arrive(i):
         @pl.when(z_gets)
@@ -519,32 +537,39 @@
         at = pl.ds(row_of(i) + half_rows * (1 - c), half_rows)
         return remote(product_ref.at[at], other2_ref.at[at], (f_s, f_r), i, here.partner())
 
+    new_stride = new_ref.shape[0] // depth
+    new3 = new_ref.reshape(depth, new_stride, width_x)
+
+    def my_half(i):
+        return pl.ds(pl.multiple_of(row_of(i) + half_rows * c, 8), half_rows)
+
     def gather(i, kind):
         oa, ob = here.others()[kind]
         return remote(
-            other2_ref.at[pl.ds(row_of(i) + half_rows * c, half_rows), pl.ds(pl.multiple_of(planes * ob, 8), planes)],
-            all_ref.at[pl.ds(rows * strip + row_of(i) + half_rows * c, half_rows)],
+            new3.at[pl.ds(planes * ob, planes), my_half(i)],
+            all_ref.at[:, pl.ds(pl.multiple_of(rows * strip + my_half(i).start, 8), half_rows)],
             (g_s, g_r), 3 * i + kind, here.device(a=oa, b=ob),
         )
 
     def own(i):
         return remote(
-            other2_ref.at[pl.ds(row_of(i) + half_rows * c, half_rows), pl.ds(pl.multiple_of(planes * b, 8), planes)],
-            all_ref.at[pl.ds(rows * strip + row_of(i) + half_rows * c, half_rows)],
+            new3.at[pl.ds(planes * b, planes), my_half(i)],
+            all_ref.at[:, pl.ds(pl.multiple_of(rows * strip + my_half(i).start, 8), half_rows)],
             (o_s, o_r), i, here.partner(),
         )
 
     def onward(i, kind):
         theirs = here.strip_of(*here.others()[kind])
         chunk = jnp.where(ascends(theirs), i - 1, chunks - i)
-        at = pl.ds(rows * theirs + reach * chunk + half_rows * c, half_rows)
-        return remote(all_ref.at[at], all_ref.at[at], (w_s, w_r), 3 * i + kind, here.partner())
+        at = pl.ds(pl.multiple_of(rows * theirs + reach * chunk + half_rows * c, 8), half_rows)
+        return remote(all_ref.at[:, at], all_ref.at[:, at], (w_s, w_r), 3 * i + kind, here.partner())
 
     def last_update():
 
+        def free(i):
+            swap(i).wait_send()
+
         def make(i):
-            swap(i).wait_send()
-            back_rows(row_of(i), reach, lzb_ref, s_ref, product_ref)
             last_swap(i).start()
 
         def use(i):
@@ -554,19 +579,30 @@
             def _(r):
                 row = row_of(i) + half_rows * c + r
                 factor = root(product_ref[row] * other2_ref[row])
-                other2_ref[row] = est2_ref[reach + row, inside] * factor
-                all_ref[rows * strip + row] = other2_ref[row, pl.ds(pl.multiple_of(planes * b, 8), planes)]
+                new_ref[pl.ds(row, depth, stride=new_stride)] = est2_ref[reach + row, inside] * factor
 
             for kind in (2, 0, 1):
                 gather(i, kind).start()
             own(i).start()
 
-        return make, use
-
-    make, use = last_update()
+            @pl.loop(0, planes, unroll=8)
+            def _(z):
+                at = pl.ds(pl.multiple_of(rows * strip + my_half(i).start, 8), half_rows)
+                all_ref[z, at] = new3[planes * b + z, my_half(i)]
+
+        return free, make, use
+
+    free, make, use = last_update()
+
+    def make_part(part):
+        ratio_part(part, t2_ref)
+        places(part, free)
+        back_part(part)
+        places(part, make)
+
     for part in range(2, parts):
         edges_come(part)
-    early = 2 * (parts - 1) - 1
+    early = 1 + starts[parts - 2]
     for part in range(parts - 1):
         rest_comes(part)
         first_update(part)
@@ -574,24 +610,21 @@
     pl.loop(1, early)(forward)
     rest_comes(parts - 1)
     first_update(parts - 1)
-    pl.loop(early, chunks - 1)(arrive)
+    pl.loop(early, late)(arrive)
     arrive_side(0, has_first)
-    pl.loop(early, chunks - 1)(forward)
+    pl.loop(early, late)(forward)
     side_forward(0, has_first)
     for part in range(parts - 2):
-        ratio_part(part, t2_ref)
-        places(part, make)
-    pl.loop(chunks - 1, chunks + 1)(arrive)
+        make_part(part)
+    pl.loop(late, chunks + 1)(lambda i: arrive(late + chunks - i))
     for part in range(parts - 2):
         places(part, use)
-    pl.loop(chunks - 1, chunks + 1)(forward)
-    ratio_part(parts - 2, t2_ref)
-    places(parts - 2, make)
+    pl.loop(late, chunks + 1)(forward)
+    make_part(parts - 2)
     arrive_side(1, has_last)
     places(parts - 2, use)
     side_forward(1, has_last)
-    ratio_part(parts - 1, t2_ref)
-    places(parts - 1, make)
+    make_part(parts - 1)
     places(parts - 1, use)
 
     @pl.loop(1, chunks + 1)
@@ -626,11 +659,10 @@
 
 
 def output_kernel(all_ref, out_ref):
-    group, lanes, width = out_ref.shape
-    stride = all_ref.shape[0] // width
+    group = out_ref.shape[0]
     base = pl.program_id(0) * group
     for i in range(group):
-        out_ref[i] = all_ref[pl.ds(base + i, width, stride=stride)].T
+        out_ref[i] = all_ref[base + i].T
 
 
 def on_device(blocks, views_data, start, psf_table, psf_index):
@@ -643,14 +675,19 @@
     wide, deep = rows + 2 * reach, depth + 2 * reach
     tall, outer = rows + 2 * pad, depth + 2 * pad
     chunks = rows // reach
-    size = 2 * reach
-    parts = rows // size
+    sizes = part_sizes(chunks)
+    parts = len(sizes)
+    y_matrices = []
+    for size in sizes:
+        own, mid, far = (reach * (size + more) for more in range(3))
+        y_matrices.append(pltpu.VMEM((2, 2 * mid, 2 * far), bf16))
+        y_matrices.append(pltpu.VMEM((2, 2 * own, 2 * mid), bf16))
     dma = lambda n: [pltpu.SemaphoreType.DMA((n,)), pltpu.SemaphoreType.DMA((n,))]
 
     by_row = jnp.transpose(psf_table, (1, 0, 2))
     gathered = pl.pallas_call(
         functools.partial(whole_kernel, blocks, rows),
-        out_shape=jax.ShapeDtypeStruct((width_y, planes, width_x), f32),
+        out_shape=jax.ShapeDtypeStruct((planes, width_y, width_x), f32),
         in_specs=[HBM, HBM, HBM, pl.BlockSpec(memory_space=pltpu.SMEM)],
         out_specs=VMEM,
         scratch_shapes=[
@@ -663,8 +700,6 @@
             pltpu.VMEM((2, outer, tall, width_x), f32),
             pltpu.VMEM((2, 2 * outer, 2 * deep), bf16),
             pltpu.VMEM((2, 2 * width_x, 2 * width_x), bf16),
-            pltpu.VMEM((2, 2 * (size + 2 * pad), 2 * (size + 2 * reach)), bf16),
-            pltpu.VMEM((2, 2 * size, 2 * (size + 2 * pad)), bf16),
             pltpu.VMEM((2, 2 * width_x, 2 * width_x), bf16),
             pltpu.VMEM((2, 2 * depth, 2 * outer), bf16),
             pltpu.VMEM((2 * wide * odd_stride(outer), width_x), f32),
@@ -673,6 +708,8 @@
             pltpu.VMEM((rows, depth, width_x), f32),
             pltpu.VMEM((rows, depth, width_x), f32),
             pltpu.VMEM((rows, depth, width_x), f32),
+            pltpu.VMEM((depth * odd_stride(rows), width_x), f32),
+            *y_matrices,
             pltpu.SemaphoreType.DMA((2 * (planes // pad) + 1,)),
             *dma(1), *dma(6 + planes // pad), *dma(6 * parts), *dma(4 * parts),
             *dma(chunks + 1), *dma(4), *dma(chunks + 1), *dma(chunks + 4),
@@ -684,12 +721,12 @@
     )(views_data[0], start, by_row, psf_index)
     return pl.pallas_call(
         output_kernel,
-        grid=(planes // 4,),
+        grid=(planes // 8,),
         out_shape=jax.ShapeDtypeStruct(start.shape, f32),
         in_specs=[VMEM],
-        out_specs=pl.BlockSpec((4, width_x, width_y), lambda i: (i, 0, 0)),
+        out_specs=pl.BlockSpec((8, width_x, width_y), lambda i: (i, 0, 0)),
         compiler_params=pltpu.CompilerParams(vmem_limit_bytes=12 * MIB),
-    )(gathered.reshape(width_y * planes, width_x))
+    )(gathered)
 
 
 def solution(mesh):

time: 101 us -> 101 us (level)
  no operation moved by 1% of the time
where the time goes in v6:
time: 101 us; the launch traced here: 100 us
  Pallas kernels  99.1 us (98%)
    pallas_call x1, Pallas kernels, on_device(): pl.pallas_call(functools.partial(whole_kernel, blocks, rows), out_shape=j...  96.9 us
    pallas_call x1, Pallas kernels, on_device(): pl.pallas_call(output_kernel, grid=(planes // 8,), out_shape=jax.ShapeDty...  2.16 us

profile of v6, /device:TPU:17, one launch (start us, length us, event | category | flops | bytes accessed | tf_op | source)
XLA Modules:
  0.0 100.5 jit_solution(16563893725301887915)
XLA Ops:
  0.7 0.0 copy-start
  0.7 0.7 copy-done
  1.4 96.9 %shard_map.46.all_ref = f32[16,384,128]{2,1,0:T(8,128)S(1)} custom-call(f32[16,128,384]{2,1,0:T(8,128)} %bitcast.3, f32[16,128,384]{2,1,0:T(8,128)} %start_hbm.1, f32[3,8,17]{2,1,0:T(8,128)S(1)} %bitcast.2, s32[1]{0:T(128)S(6)} %copy.5.index_ref), custom_call_target="tpu_custom_call" | custom-call | tf_op jit(solution)/shard_map/pallas_call | solution.py:688
  98.3 2.2 %shard_map.47 = f32[16,128,384]{2,1,0:T(8,128)} custom-call(f32[16,384,128]{2,1,0:T(8,128)S(1)} %shard_map.46.all_ref), custom_call_target="tpu_custom_call" | custom-call | tf_op jit(solution)/shard_map/pallas_call | solution.py:722
Async XLA Ops:
  0.7 0.7 copy-start
